TPU v7x, 32 devices: a whole 2x2x4 slice. The times are simulated.
32 devices in a mesh: dp: 2 (over y), tm: 4 (over z), rows: 4 (over x, core).
Axes of the slice: x: 2, y: 2, z: 4, core: 2. Of those that a mesh axis runs over, the one named last changes fastest.
Arguments:
- clips: bfloat16 [2, 8, 4, 128, 256], P('dp', 'tm', 'rows'), may hold values from -12 to 12
- weight: bfloat16 [3, 3, 3, 256, 256], replicated, may hold values from -0.078125 to 0.078125
- bias: float32 [256], replicated, may hold values from -1 to 1
- head: float32 [256], replicated, may hold values from -4 to 4
Outputs:
- grad_weight: float32 [3, 3, 3, 256, 256], replicated
- grad_bias: float32 [256], replicated
- grad_head: float32 [256], replicated
All inputs are finite; a program needn't handle non-finite values.
Results may differ from a plain program's by a relative error of at most 0.0003.
Values may be sent and summed in bfloat16 or wider, within the bound.
A program may use at most 128 MiB of HBM per device.

v0:
```python
import functools
import math

import jax
import jax.numpy as jnp
from jax import lax
from jax.experimental import pallas as pl
from jax.experimental.pallas import tpu as pltpu
from jax.sharding import PartitionSpec as P

penalty_weight = 0.01
MESH = pl.DeviceIdType.MESH
SUB = 8
TAPS = 3
SPAN = 120.0


def make_plan(sizes, shares):
    dp, tm, rows = sizes
    cuts, rest, left = [], [], shares
    near = 2 if rows % 2 == 0 else 1
    for axis, stride, count in (("rows", 1, near), ("rows", near, rows // near), ("dp", 1, dp), ("tm", 1, tm)):
        cut = 1
        while count % (2 * cut) == 0 and left % (2 * cut) == 0:
            cut *= 2
        left //= cut
        cuts.append((axis, stride, cut))
        rest.append((axis, stride * cut, count // cut))
    pair, far, depth, line = cuts
    rest = tuple(group for group in rest if group[2] > 1)
    across, along, ahead = (far, depth, line), (depth, far, line), (line, depth, far)
    between = (depth, line, far)
    return pair, (ahead, along, across, between, across, along), rest


def kernel(
    sizes, plan, clips_ref, weight_ref, bias_ref, head_ref,
    out_ref, bias_out, head_out,
    w_ref, clip_pad, score_pad, grad_pad, acc, slope_ref, curve_ref, cat_s, cat_p, total,
    land_pair, code, land, full, small_mine, small_land,
    local_sem, halo_send, halo_recv, pair_send, pair_recv, part_send, part_recv, gath_send, gath_recv,
    small_send, small_recv, out_sem,
):
    small_refs = (bias_out, head_out)
    dp, tm, rows = sizes
    frames, cols, chans = clips_ref.shape
    count = frames * cols
    me = {"dp": lax.axis_index("dp"), "tm": lax.axis_index("tm"), "rows": lax.axis_index("rows")}

    def device(**moved):
        place = dict(me, **moved)
        return (place["dp"], place["tm"], place["rows"])

    weight_copy = pltpu.make_async_copy(weight_ref, w_ref, local_sem.at[0])
    weight_copy.start()
    clip_copy = pltpu.make_async_copy(
        clips_ref, clip_pad.at[pl.ds(1, frames), 1], local_sem.at[1]
    )
    clip_copy.start()
    for pad in (clip_pad, score_pad, grad_pad):
        pad[:, 0] = jnp.zeros((frames + 2, cols, chans), pad.dtype)
        pad[:, 2] = jnp.zeros((frames + 2, cols, chans), pad.dtype)
        pad[0, 1] = jnp.zeros((cols, chans), pad.dtype)
        pad[frames + 1, 1] = jnp.zeros((cols, chans), pad.dtype)

    barrier = pltpu.get_barrier_semaphore()
    flat = me["tm"] * rows + me["rows"]
    plane = tm * rows

    def greet(step, carry):
        other = lax.rem(flat + step, plane)
        pl.semaphore_signal(
            barrier, inc=1, device_id=device(tm=other // rows, rows=lax.rem(other, rows)),
            device_id_type=MESH,
        )
        return carry

    lax.fori_loop(1, plane, greet, 0)
    for step in range(1, dp):
        pl.semaphore_signal(
            barrier, inc=1, device_id=device(dp=lax.rem(me["dp"] + step, dp)), device_id_type=MESH
        )
    pl.semaphore_wait(barrier, plane - 1 + dp - 1)

    moves = [(t, r) for t in (-1, 0, 1) for r in (-1, 0, 1) if (t, r) != (0, 0)]

    def inside(t, r):
        ok = None
        for axis, step, size in (("tm", t, tm), ("rows", r, rows)):
            if step:
                cond = me[axis] > 0 if step < 0 else me[axis] < size - 1
                ok = cond if ok is None else jnp.logical_and(ok, cond)
        return ok

    def halo_copy(which, pad, source, t, r):
        slot = which * len(moves) + moves.index((t, r))
        if t == 0:
            here, there = pl.ds(0, frames), pl.ds(1, frames)
        elif t > 0:
            here, there = pl.ds(frames - 1, 1), pl.ds(0, 1)
        else:
            here, there = pl.ds(0, 1), pl.ds(frames + 1, 1)
        return pltpu.make_async_remote_copy(
            src_ref=source.at[here], dst_ref=pad.at[there, 1 - r],
            send_sem=halo_send.at[slot], recv_sem=halo_recv.at[slot],
            device_id=device(tm=me["tm"] + t, rows=me["rows"] + r), device_id_type=MESH,
        )

    def halo_start(which, pad, source):
        for t, r in moves:
            @pl.when(inside(t, r))
            def _():
                halo_copy(which, pad, source, t, r).start()

    def halo_wait(which, pad, source, level):
        for t, r in moves:
            if (t == 0) != level:
                continue

            @pl.when(inside(t, r))
            def _():
                halo_copy(which, pad, source, t, r).wait_send()

            @pl.when(inside(-t, -r))
            def _():
                halo_copy(which, pad, source, t, r).wait_recv()

    column = lax.rem(lax.broadcasted_iota(jnp.int32, (count, chans), 0), cols)

    def earlier(value):
        return jnp.where(column == 0, 0.0, pltpu.roll(value, 1, 0))

    def later(value):
        return jnp.where(column == cols - 1, 0.0, pltpu.roll(value, count - 1, 0))

    def conv(which, pad, source, transpose):
        def step(a):
            base = (TAPS - 1 - a) if transpose else a
            pieces = [
                pad[pl.ds(base, frames), (TAPS - 1 - b) if transpose else b].reshape(count, chans)
                for b in range(TAPS)
            ]
            left = jnp.concatenate(pieces, axis=1)
            for d in range(TAPS):
                taps = [w_ref[(a * TAPS + b) * TAPS + d] for b in range(TAPS)]
                if transpose:
                    part = lax.dot_general(
                        left, jnp.concatenate(taps, axis=1), (((1,), (1,)), ((), ())),
                        preferred_element_type=jnp.float32,
                    )
                else:
                    part = jnp.dot(
                        left, jnp.concatenate(taps, axis=0), preferred_element_type=jnp.float32
                    )
                acc[d] = part if a == 1 else acc[d] + part

        halo_wait(which, pad, source, True)
        step(1)
        halo_wait(which, pad, source, False)
        step(0)
        step(2)
        if transpose:
            return later(acc[0]) + acc[1] + earlier(acc[2])
        return earlier(acc[0]) + acc[1] + later(acc[2])

    def shifted(value):
        value = value.astype(jnp.float32)
        return jnp.concatenate(
            [later(value), value, earlier(value)], axis=1
        ).astype(jnp.bfloat16)

    halo_start(0, clip_pad, clips_ref)
    clip_copy.wait()
    weight_copy.wait()
    pre = conv(0, clip_pad, clips_ref, False) + bias_ref[...]
    sig = jax.nn.sigmoid(pre)
    slope = sig * (1.0 + pre * (1.0 - sig))
    slope_ref[...] = slope
    curve_ref[...] = sig * (1.0 - sig) * (2.0 + pre * (1.0 - 2.0 * sig))
    score = (head_ref[...] * slope).astype(jnp.bfloat16)
    score_pad[pl.ds(1, frames), 1] = score.reshape(frames, cols, chans)
    score_own = score_pad.at[pl.ds(1, frames), 1]
    cat_s[...] = shifted(score)
    halo_start(1, score_pad, score_own)

    input_grad = conv(1, score_pad, score_own, True).astype(jnp.bfloat16)
    grad_pad[pl.ds(1, frames), 1] = input_grad.reshape(frames, cols, chans)
    grad_own = grad_pad.at[pl.ds(1, frames), 1]
    halo_start(2, grad_pad, grad_own)

    back = penalty_weight * conv(2, grad_pad, grad_own, False)
    pre_grad = back * head_ref[...] * curve_ref[...]
    cat_p[...] = shifted(pre_grad.astype(jnp.bfloat16))
    small_mine[...] = jnp.zeros_like(small_mine)
    small_mine[pl.ds(0, 1)] = jnp.sum(pre_grad, axis=0, keepdims=True)
    small_mine[pl.ds(1, 1)] = jnp.sum(back * slope_ref[...], axis=0, keepdims=True)

    pair, orders, rest = plan
    parts, shares, taps = total.shape[:3]
    lanes = land.shape[-1]
    split = chans // lanes
    half = shares // pair[2]
    units = chans // SUB

    def place_in(group):
        axis, stride, size = group
        return lax.rem(me[axis] // stride, size)

    def peer(group, step):
        axis, stride, size = group
        mine = place_in(group)
        other = lax.rem(mine + step, size)
        return other, device(**{axis: me[axis] + (other - mine) * stride})

    def pair_copy(a):
        other, target = peer(pair, 1)
        here = pl.ds(a * split, split)
        return pltpu.make_async_remote_copy(
            src_ref=total.at[here, pl.ds(other * half, half)], dst_ref=land_pair.at[here],
            send_sem=pair_send.at[a], recv_sem=pair_recv.at[a],
            device_id=target, device_id_type=MESH,
        )

    def correlate(a):
        def step(b, carry):
            dims = (((0,), (0,)), ((), ()))
            first = lax.dot_general(
                grad_pad[a : a + frames, b].reshape(count, chans), cat_s[...], dims,
                preferred_element_type=jnp.float32,
            )
            second = lax.dot_general(
                clip_pad[a : a + frames, b].reshape(count, chans), cat_p[...], dims,
                preferred_element_type=jnp.float32,
            )
            both = penalty_weight * first + second
            for d in range(TAPS):
                for p in range(split):
                    at = d * chans + p * lanes
                    total[a * split + p, :, b * TAPS + d] = both[:, at : at + lanes].reshape(
                        units, SUB, lanes
                    )
            return carry

        lax.fori_loop(0, TAPS, step, 0)
        if pair[2] > 1:
            pair_copy(a).start()

    def finish_pair(a):
        if pair[2] == 1:
            return
        mine = place_in(pair) * half
        pair_copy(a).wait()

        def add(step, carry):
            for p in range(a * split, (a + 1) * split):
                total[p, mine + step] = total[p, mine + step] + land_pair[p, step]
            return carry

        lax.fori_loop(0, half, add, 0)

    def encode(value):
        top = (jnp.max(jnp.abs(value), axis=0) * 1.01 + 1e-30).astype(jnp.bfloat16)
        rate = SPAN / top.astype(jnp.float32)
        return jnp.exp2(value * rate[None]).astype(jnp.bfloat16), top

    sems = {"part": 0, "gath": 0, "land": 0}

    def scatter_start(p, group, base, size, whole=False):
        share = size if whole else size // group[2]
        copies = []
        for step in range(1, group[2]):
            other, target = peer(group, step)
            origin = base if whole else base + other * share
            at = sems["land"]

            def fill(k, carry):
                value, top = encode(total[p, origin + k])
                code[at + k, pl.ds(0, taps)] = value
                code[at + k, taps] = top
                return carry

            lax.fori_loop(0, share, fill, 0)
            copy = pltpu.make_async_remote_copy(
                src_ref=code.at[pl.ds(at, share)], dst_ref=land.at[pl.ds(at, share)],
                send_sem=part_send.at[sems["part"]], recv_sem=part_recv.at[sems["part"]],
                device_id=target, device_id_type=MESH,
            )
            copy.start()
            copies.append((copy, at))
            sems["land"] += share
            sems["part"] += 1
        return copies, base if whole else base + place_in(group) * share, share

    def scatter_end(p, copies, base, share):
        for copy, _ in copies:
            copy.wait()
        if not copies:
            return

        def add(step, carry):
            value = total[p, base + step]
            for _, at in copies:
                value = value + decode(land[at + step], taps)
            total[p, base + step] = value
            return carry

        lax.fori_loop(0, share, add, 0)

    def gather_start(p, group, base, size):
        copies = []
        for step in range(1, group[2]):
            _, target = peer(group, step)
            block = full.at[p, pl.ds(base, size)]
            copy = pltpu.make_async_remote_copy(
                src_ref=block, dst_ref=block,
                send_sem=gath_send.at[sems["gath"]], recv_sem=gath_recv.at[sems["gath"]],
                device_id=target, device_id_type=MESH,
            )
            copy.start()
            copies.append(copy)
            sems["gath"] += 1
        return copies

    base = place_in(pair) * half
    state = [(base, half)] * parts
    trail = [[] for _ in range(parts)]
    started = [None] * parts
    depth = len(orders[0])

    def small_start(number, group, at):
        copies = []
        for step in range(1, group[2]):
            _, target = peer(group, step)
            copy = pltpu.make_async_remote_copy(
                src_ref=small_mine.at[pl.ds(number * SUB, SUB)],
                dst_ref=small_land.at[pl.ds(at * SUB, SUB)],
                send_sem=small_send.at[at], recv_sem=small_recv.at[at],
                device_id=target, device_id_type=MESH,
            )
            copy.start()
            copies.append((copy, at))
            at += 1
        return copies

    def small_end(number, copies):
        value = small_mine[pl.ds(number * SUB, SUB)]
        for copy, _ in copies:
            copy.wait()
        for _, slot in copies:
            value = value + small_land[pl.ds(slot * SUB, SUB)]
        small_mine[pl.ds((number + 1) * SUB, SUB)] = value

    def scatter(p, level):
        if level < depth:
            trail[p].append(state[p])
            started[p] = scatter_start(p, orders[p][level], *state[p])
        else:
            started[p] = scatter_start(p, rest[level - depth], *state[p], True)

    def end_scatter(p):
        copies, base, share = started[p]
        scatter_end(p, copies, base, share)
        state[p] = (base, share)

    small_groups = (pair, *orders[0], *rest)
    small_at = 0
    for a in range(TAPS):
        correlate(a)
        if a == 0:
            small = small_start(0, small_groups[0], small_at)
            small_at += len(small)
        else:
            finish_pair(a - 1)
            for p in range((a - 1) * split, a * split):
                scatter(p, 0)
    small_end(0, small)
    finish_pair(TAPS - 1)
    for p in range(parts - split, parts):
        scatter(p, 0)
    levels = depth + len(rest)
    for level in range(1, levels + 1):
        small = small_start(level, small_groups[level], small_at)
        small_at += len(small)
        for p in range(parts):
            end_scatter(p)
            if level < levels:
                scatter(p, level)
                continue
            base, size = state[p]

            def keep(k, carry):
                value, top = encode(total[p, base + k])
                full[p, base + k, pl.ds(0, taps)] = value
                full[p, base + k, taps] = top
                return carry

            lax.fori_loop(0, size, keep, 0)
            started[p] = gather_start(p, orders[p][depth - 1], *state[p])
        small_end(level, small)
    for k in range(2):
        small_refs[k][...] = small_mine[pl.ds((levels + 1) * SUB + k, 1)]
    for level in reversed(range(depth)):
        for p in range(parts):
            for copy in started[p]:
                copy.wait()
            state[p] = trail[p][level]
            group = orders[p][level - 1] if level else pair
            started[p] = gather_start(p, group, *state[p])
    outs = []
    for p in range(parts):
        for copy in started[p]:
            copy.wait()
        copy = pltpu.make_async_copy(full.at[p], out_ref.at[p], out_sem.at[p])
        copy.start()
        outs.append(copy)
    for copy in outs:
        copy.wait()


def decode(block, taps):
    unit = block[taps].astype(jnp.float32) * (1.0 / (SPAN * math.log(2.0)))
    return jnp.log(block[:taps].astype(jnp.float32)) * unit[None]


def decode_kernel(code_ref, bias_ref, head_ref, out_ref, bias_out, head_out):
    parts, shares, blocks, _, lanes = code_ref.shape
    taps = blocks - 1
    split = parts // TAPS
    for p in range(parts):
        at, lane = p // split * taps, p % split * lanes
        for k in range(shares):
            out_ref[at : at + taps, k, :, lane : lane + lanes] = decode(code_ref[p, k], taps)
    bias_out[...] = bias_ref[...]
    head_out[...] = head_ref[...]


def per_device(sizes, clips, weight, bias, head):
    _, frames, _, cols, chans = clips.shape
    count = frames * cols
    split = 2
    taps, shares, parts = TAPS**2, chans // SUB, TAPS * split
    lanes = chans // split
    plan = make_plan(sizes, shares)
    pair, orders, rest = plan
    half = shares // pair[2]
    small_n = sum(g[2] - 1 for g in (pair,) + orders[0] + rest)
    land = parts_n = gath_n = 0
    for order in orders:
        size = half
        for group in order:
            land += size // group[2] * (group[2] - 1)
            size //= group[2]
            parts_n += group[2] - 1
        for group in rest:
            land += size * (group[2] - 1)
            parts_n += group[2] - 1
        gath_n += sum(g[2] - 1 for g in order) + pair[2] - 1
    pad = pltpu.VMEM((frames + 2, 3, cols, chans), jnp.bfloat16)
    field = pltpu.VMEM((count, chans), jnp.float32)
    coded = pltpu.VMEM((max(land, 1), taps + 1, SUB, lanes), jnp.bfloat16)
    dma = pltpu.SemaphoreType.DMA
    vmem = pl.BlockSpec(memory_space=pltpu.VMEM)
    hbm = pl.BlockSpec(memory_space=pl.ANY)
    row = jax.ShapeDtypeStruct((1, chans), jnp.float32)
    code, *small = pl.pallas_call(
        functools.partial(kernel, sizes, plan),
        out_shape=(
            jax.ShapeDtypeStruct((parts, shares, taps + 1, SUB, lanes), jnp.bfloat16),
            row, row,
        ),
        in_specs=[hbm, hbm, vmem, vmem],
        out_specs=(hbm, vmem, vmem),
        scratch_shapes=[
            pltpu.VMEM((TAPS**3, chans, chans), jnp.bfloat16),
            pad, pad, pad,
            pltpu.VMEM((TAPS, count, chans), jnp.float32),
            field, field,
            pltpu.VMEM((count, TAPS * chans), jnp.bfloat16),
            pltpu.VMEM((count, TAPS * chans), jnp.bfloat16),
            pltpu.VMEM((parts, shares, taps, SUB, lanes), jnp.float32),
            pltpu.VMEM((parts, half, taps, SUB, lanes), jnp.float32),
            coded, coded,
            pltpu.VMEM((parts, shares, taps + 1, SUB, lanes), jnp.bfloat16),
            pltpu.VMEM(((len(rest) + 6) * SUB, chans), jnp.float32),
            pltpu.VMEM((max(small_n, 1) * SUB, chans), jnp.float32),
            dma((2,)), dma((24,)), dma((24,)), dma((TAPS,)), dma((TAPS,)),
            dma((max(parts_n, 1),)), dma((max(parts_n, 1),)),
            dma((max(gath_n, 1),)), dma((max(gath_n, 1),)),
            dma((max(small_n, 1),)), dma((max(small_n, 1),)), dma((parts,)),
        ],
        compiler_params=pltpu.CompilerParams(
            collective_id=0, has_side_effects=True, vmem_limit_bytes=60 * 1024 * 1024
        ),
    )(
        clips.reshape(frames, cols, chans),
        weight.reshape(TAPS**3, chans, chans),
        bias.reshape(1, chans),
        head.reshape(1, chans),
    )
    step = math.gcd(shares, 8)
    short = pl.BlockSpec((1, chans), lambda i: (0, 0))
    grad_weight, grad_bias, grad_head = pl.pallas_call(
        decode_kernel,
        out_shape=(jax.ShapeDtypeStruct((TAPS**3, shares, SUB, chans), jnp.float32), row, row),
        grid=(shares // step,),
        in_specs=[
            pl.BlockSpec((parts, step, taps + 1, SUB, lanes), lambda i: (0, i, 0, 0, 0)),
            short, short,
        ],
        out_specs=(
            pl.BlockSpec((TAPS**3, step, SUB, chans), lambda i: (0, i, 0, 0)), short, short
        ),
    )(code, *small)
    grad_weight = grad_weight.reshape(TAPS, TAPS, TAPS, chans, chans)
    return grad_weight, grad_bias.reshape(chans), grad_head.reshape(chans)


def solution(mesh):
    sizes = tuple(mesh.shape[axis] for axis in ("dp", "tm", "rows"))
    return jax.shard_map(
        functools.partial(per_device, sizes),
        mesh=mesh,
        in_specs=(P("dp", "tm", "rows", None, None), P(), P(), P()),
        out_specs=(P(), P(), P()),
        check_vma=False,
    )
```

profile of v0, /device:TPU:0, one launch (start us, length us, event | category | flops | bytes accessed | tf_op | source)
XLA Modules:
  0.0 86.2 jit_solution(17868260394472391210)
XLA Ops:
  0.6 79.8 %shard_map.67 = (bf16[6,32,10,8,128]{4,3,2,1,0:T(8,128)(2,1)}, f32[1,256]{1,0:T(1,128)}, f32[1,256]{1,0:T(1,128)}) custom-call(bf16[2,128,256]{2,1,0:T(8,128)(2,1)} %bitcast.8, bf16[27,256,256]{2,1,0:T(8,128)(2,1)} %bitcast.7, f32[1,256]{1,0:T(1,128)} %bitcast.9, f32[1,256]{1,0:T(1,128)} %bitcast.10), custom_call_target="tpu_custom_call" | custom-call | tf_op jit(solution)/shard_map/pallas_call | solution.py:465
  80.4 5.8 %shard_map.68 = (f32[27,32,8,256]{3,2,1,0:T(8,128)}, f32[1,256]{1,0:T(1,128)}, f32[1,256]{1,0:T(1,128)}) custom-call(bf16[6,32,10,8,128]{4,3,2,1,0:T(8,128)(2,1)} %get-tuple-element.9.code_ref, f32[1,256]{1,0:T(1,128)} %get-tuple-element.10.bias_ref, f32[1,256]{1,0:T(1,128)} %get-tuple-element.11.head_ref), custom_call_target="tpu_custom_call" | custom-call | tf_op jit(solution)/shard_map/pallas_call | solution.py:502
where the time goes:
time: 86.5 us; the launch traced here: 86.2 us
  Pallas kernels  85.6 us (99%)
    pallas_call x1, Pallas kernels, per_device(): pl.pallas_call(functools.partial(kernel, sizes, plan), out_shape=(jax.Sha...  79.8 us
    pallas_call x1, Pallas kernels, per_device(): pl.pallas_call(decode_kernel, out_shape=(jax.ShapeDtypeStruct((TAPS ** 3,...  5.79 us

commit v1 on v0

v1 whole, which is shorter than its diff:
```python
import functools
import math

import jax
import jax.numpy as jnp
from jax import lax
from jax.experimental import pallas as pl
from jax.experimental.pallas import tpu as pltpu
from jax.sharding import PartitionSpec as P

penalty_weight = 0.01
MESH = pl.DeviceIdType.MESH
SUB = 8
TAPS = 3
SPAN = 120.0
LANES = 128


def split_line(tm, most):
    line = 1
    while tm % (2 * line) == 0 and 2 * line <= most:
        line *= 2
    return line, tm // line


def decode(block, taps):
    unit = block[taps].astype(jnp.float32) * (1.0 / (SPAN * math.log(2.0)))
    return jnp.log(block[:taps].astype(jnp.float32)) * unit[None]


def encode(value):
    top = (jnp.max(jnp.abs(value), axis=0) * 1.01 + 1e-30).astype(jnp.bfloat16)
    rate = SPAN / top.astype(jnp.float32)
    return jnp.exp2(value * rate[None]).astype(jnp.bfloat16), top


def kernel(
    sizes, line, clips_ref, weight_ref, bias_ref, head_ref,
    out_ref, bias_out, head_out,
    w_ref, clip_pad, score_pad, grad_pad, acc, slope_ref, curve_ref,
    clip_all, grad_all, turned, slices, shifts, first, total, code, land, more, full,
    small_mine, small_plane, small_line,
    local_sem, halo_send, halo_recv, all_send, all_recv, pass_send, pass_recv,
    slice_send, slice_recv, part_send, part_recv, more_send, more_recv,
    line_send, line_recv, near_send, near_recv, turn_send, turn_recv, pair_send, pair_recv,
    sum_send, sum_recv, end_send, end_recv,
):
    dp, tm, rows = sizes
    frames, cols, chans = clips_ref.shape
    count = frames * cols
    plane = dp * rows
    share = chans // plane
    part = share // line
    taps = TAPS**2
    pair = 2 if rows % 2 == 0 else 1
    near = rows // pair
    me = {"dp": lax.axis_index("dp"), "tm": lax.axis_index("tm"), "rows": lax.axis_index("rows")}
    mine = me["dp"] * rows + me["rows"]

    def device(**moved):
        place = dict(me, **moved)
        return (place["dp"], place["tm"], place["rows"])

    def shift(axis, step):
        return lax.rem(me[axis] + step % dict(dp=dp, tm=tm, rows=rows)[axis], dict(dp=dp, tm=tm, rows=rows)[axis])

    def remote(src, dst, send, recv, target):
        return pltpu.make_async_remote_copy(
            src_ref=src, dst_ref=dst, send_sem=send, recv_sem=recv,
            device_id=target, device_id_type=MESH,
        )

    weight_copy = pltpu.make_async_copy(weight_ref, w_ref, local_sem.at[0])
    weight_copy.start()
    clip_copy = pltpu.make_async_copy(
        clips_ref, clip_pad.at[pl.ds(1, frames), 1], local_sem.at[1]
    )
    clip_copy.start()

    steps = {(i, t % tm, s) for i in range(dp) for t in (-1, 0, 1) for s in range(rows)}
    steps |= {(0, t, 0) for t in range(tm)}
    steps = sorted(steps - {(0, 0, 0)})
    barrier = pltpu.get_barrier_semaphore()
    for i, t, s in steps:
        pl.semaphore_signal(
            barrier, inc=1, device_id=(shift("dp", i), shift("tm", t), shift("rows", s)),
            device_id_type=MESH,
        )
    for axis, bound, fill in (
        ("rows", 0, lambda pad: pad.at[:, 0]), ("rows", rows - 1, lambda pad: pad.at[:, 2]),
        ("tm", 0, lambda pad: pad.at[0]), ("tm", tm - 1, lambda pad: pad.at[frames + 1]),
    ):
        @pl.when(me[axis] == bound)
        def _():
            for pad in (clip_pad, score_pad, grad_pad):
                at = fill(pad)
                at[...] = jnp.zeros(at.shape, at.dtype)
    for which in range(2):
        for edge in (0, rows + 1):
            shifts[which, :, edge] = jnp.zeros(shifts.shape[1:2] + shifts.shape[3:], shifts.dtype)
        for edge, bound in ((0, 0), (frames + 1, tm - 1)):
            @pl.when(me["tm"] == bound)
            def _():
                slices[which, :, edge] = jnp.zeros((plane, share, cols), slices.dtype)
    pl.semaphore_wait(barrier, len(steps))

    moves = [(t, r) for t in (-1, 0, 1) for r in (-1, 0, 1) if (t, r) != (0, 0)]

    def inside(t, r):
        ok = None
        for axis, step, size in (("tm", t, tm), ("rows", r, rows)):
            if step:
                cond = me[axis] > 0 if step < 0 else me[axis] < size - 1
                ok = cond if ok is None else jnp.logical_and(ok, cond)
        return ok

    def halo_copy(which, pad, source, t, r):
        slot = which * len(moves) + moves.index((t, r))
        if t == 0:
            here, there = pl.ds(0, frames), pl.ds(1, frames)
        elif t > 0:
            here, there = pl.ds(frames - 1, 1), pl.ds(0, 1)
        else:
            here, there = pl.ds(0, 1), pl.ds(frames + 1, 1)
        return pltpu.make_async_remote_copy(
            src_ref=source.at[here], dst_ref=pad.at[there, 1 - r],
            send_sem=halo_send.at[slot], recv_sem=halo_recv.at[slot],
            device_id=device(tm=me["tm"] + t, rows=me["rows"] + r), device_id_type=MESH,
        )

    def halo_start(which, pad, source):
        for t, r in moves:
            @pl.when(inside(t, r))
            def _():
                halo_copy(which, pad, source, t, r).start()

    def halo_wait(which, pad, source, level):
        for t, r in moves:
            if (t == 0) != level:
                continue

            @pl.when(inside(t, r))
            def _():
                halo_copy(which, pad, source, t, r).wait_send()

            @pl.when(inside(-t, -r))
            def _():
                halo_copy(which, pad, source, t, r).wait_recv()

    column = lax.rem(lax.broadcasted_iota(jnp.int32, (count, chans), 0), cols)

    def earlier(value):
        return jnp.where(column == 0, 0.0, pltpu.roll(value, 1, 0))

    def later(value):
        return jnp.where(column == cols - 1, 0.0, pltpu.roll(value, count - 1, 0))

    def conv(which, pad, source, transpose):
        def step(a):
            base = (TAPS - 1 - a) if transpose else a
            pieces = [
                pad[pl.ds(base, frames), (TAPS - 1 - b) if transpose else b].reshape(count, chans)
                for b in range(TAPS)
            ]
            left = jnp.concatenate(pieces, axis=1)
            for d in range(TAPS):
                taps = [w_ref[(a * TAPS + b) * TAPS + d] for b in range(TAPS)]
                if transpose:
                    part = lax.dot_general(
                        left, jnp.concatenate(taps, axis=1), (((1,), (1,)), ((), ())),
                        preferred_element_type=jnp.float32,
                    )
                else:
                    part = jnp.dot(
                        left, jnp.concatenate(taps, axis=0), preferred_element_type=jnp.float32
                    )
                acc[d] = part if a == 1 else acc[d] + part

        halo_wait(which, pad, source, True)
        step(1)
        halo_wait(which, pad, source, False)
        step(0)
        step(2)
        if transpose:
            return later(acc[0]) + acc[1] + earlier(acc[2])
        return earlier(acc[0]) + acc[1] + later(acc[2])


    close = [(i, s) for i in range(dp) for s in range(near) if (i, s) != (0, 0)]
    partner = me["rows"] + 1 - 2 * lax.rem(me["rows"], 2) if pair == 2 else me["rows"]

    def origin(i, s):
        return shift("dp", -i) * rows + shift("rows", -pair * s)

    def all_copy(which, buf, k):
        i, s = close[k]
        at = which * len(close) + k
        return remote(
            buf.at[mine], buf.at[mine], all_send.at[at], all_recv.at[at],
            device(dp=shift("dp", i), rows=shift("rows", pair * s)),
        )

    def pass_copy(which, buf, k):
        at = which * (len(close) + 1) + k
        block = buf.at[mine if k == len(close) else origin(*close[k])]
        return remote(block, block, pass_send.at[at], pass_recv.at[at], device(rows=partner))

    def all_start(which, buf):
        if pair == 2:
            pass_copy(which, buf, len(close)).start()
        for k in range(len(close)):
            all_copy(which, buf, k).start()

    def all_pass(which, buf):
        for k in range(len(close)):
            all_copy(which, buf, k).wait()
            if pair == 2:
                pass_copy(which, buf, k).start()

    def all_end(which, buf):
        if pair == 2:
            for k in range(len(close) + 1):
                pass_copy(which, buf, k).wait()

    def slice_copy(which, t, i, s):
        at = (which * 3 + t + 1) * plane + i * rows + s
        y, r = shift("dp", i), shift("rows", s)
        rest = pl.ds(pl.multiple_of((y * rows + r) * share, share), share)
        if t == 0:
            src, dst = turned.at[which, :, rest], slices.at[which, mine, pl.ds(1, frames)]
        elif t > 0:
            src, dst = turned.at[which, frames - 1, rest], slices.at[which, mine, 0]
        else:
            src, dst = turned.at[which, 0, rest], slices.at[which, mine, frames + 1]
        return remote(
            src, dst, slice_send.at[at], slice_recv.at[at],
            device(dp=y, rows=r, tm=me["tm"] + t),
        )

    pieces = [(i, s) for i in range(dp) for s in range(rows)]

    def slice_start(which, value):
        for f in range(frames):
            turned[which, f] = value[f * cols : (f + 1) * cols].T.astype(jnp.bfloat16)
        for t in (1, -1):
            @pl.when(inside(t, 0))
            def _():
                for i, s in pieces:
                    slice_copy(which, t, i, s).start()
        for i, s in pieces[1:]:
            slice_copy(which, 0, i, s).start()
        own = pl.ds(pl.multiple_of(mine * share, share), share)
        for f in range(frames):
            slices[which, mine, f + 1] = turned[which, f, own]

    lane = lax.broadcasted_iota(jnp.int32, (share, cols), 1)

    def slice_end(which):
        for t in (1, -1):
            @pl.when(inside(t, 0))
            def _():
                for i, s in pieces:
                    slice_copy(which, t, i, s).wait_send()

            @pl.when(inside(-t, 0))
            def _():
                for i, s in pieces:
                    slice_copy(which, t, i, s).wait_recv()
        for i, s in pieces[1:]:
            slice_copy(which, 0, i, s).wait()
        for j in range(plane):
            for f in range(frames + 2):
                value = slices[which, j, f].astype(jnp.float32)
                after = jnp.where(lane == cols - 1, 0.0, pltpu.roll(value, cols - 1, 1))
                before = jnp.where(lane == 0, 0.0, pltpu.roll(value, 1, 1))
                shifts[which, j // rows, j % rows + 1, f] = jnp.concatenate(
                    [after, value, before], axis=0
                ).astype(jnp.bfloat16)

    def correlate(which, buf, a):
        left = jnp.concatenate(
            [
                jnp.concatenate(
                    [
                        shifts[which, y, r + 2 - b, f + 2 - a]
                        for y in range(dp) for r in range(rows) for f in range(frames)
                    ],
                    axis=1,
                )
                for b in range(TAPS)
            ],
            axis=0,
        )
        right = buf[...].reshape(plane * count, chans)
        return jnp.dot(left, right, preferred_element_type=jnp.float32)

    halo_start(0, clip_pad, clips_ref)
    clip_copy.wait()
    clip_all[mine] = clip_pad[pl.ds(1, frames), 1].reshape(count, chans)
    all_start(0, clip_all)
    weight_copy.wait()
    pre = conv(0, clip_pad, clips_ref, False) + bias_ref[...]
    sig = jax.nn.sigmoid(pre)
    slope = sig * (1.0 + pre * (1.0 - sig))
    slope_ref[...] = slope
    curve_ref[...] = sig * (1.0 - sig) * (2.0 + pre * (1.0 - 2.0 * sig))
    score = (head_ref[...] * slope).astype(jnp.bfloat16)
    score_pad[pl.ds(1, frames), 1] = score.reshape(frames, cols, chans)
    score_own = score_pad.at[pl.ds(1, frames), 1]
    halo_start(1, score_pad, score_own)
    slice_start(0, score.astype(jnp.float32))
    all_pass(0, clip_all)

    input_grad = conv(1, score_pad, score_own, True).astype(jnp.bfloat16)
    grad_pad[pl.ds(1, frames), 1] = input_grad.reshape(frames, cols, chans)
    grad_own = grad_pad.at[pl.ds(1, frames), 1]
    halo_start(2, grad_pad, grad_own)
    grad_all[mine] = input_grad
    all_start(1, grad_all)
    slice_end(0)
    all_end(0, clip_all)

    back = penalty_weight * conv(2, grad_pad, grad_own, False)
    pre_grad = back * head_ref[...] * curve_ref[...]
    slice_start(1, pre_grad.astype(jnp.bfloat16).astype(jnp.float32))
    small_mine[...] = jnp.zeros_like(small_mine)
    small_mine[pl.ds(0, 1)] = jnp.sum(pre_grad, axis=0, keepdims=True)
    small_mine[pl.ds(1, 1)] = jnp.sum(back * slope_ref[...], axis=0, keepdims=True)

    def sum_copy(i, s):
        at = i * rows + s
        return remote(
            small_mine, small_plane.at[mine], sum_send.at[at], sum_recv.at[at],
            device(dp=shift("dp", i), rows=shift("rows", s)),
        )

    small_plane[mine] = small_mine[...]
    for i, s in pieces[1:]:
        sum_copy(i, s).start()

    all_pass(1, grad_all)
    all_end(1, grad_all)
    for a in range(TAPS):
        first[a] = penalty_weight * correlate(0, grad_all, a)

    slice_end(1)
    inner, outer = lax.rem(me["tm"], line), me["tm"] // line

    def along(step):
        return lax.rem(inner + step, line)

    def part_copy(a, step):
        at = a * line + step
        return remote(
            code.at[a, along(step)], land.at[a, inner], part_send.at[at], part_recv.at[at],
            device(tm=outer * line + along(step)),
        )

    def scatter(a):
        both = (first[a] + correlate(1, clip_all, a)).reshape(taps, share, chans)
        for t in range(line):
            total[a, t] = both[:, t * part : (t + 1) * part]
        for step in range(1, line):
            value, top = encode(total[a, along(step)])
            code[a, along(step), pl.ds(0, taps)] = value
            code[a, along(step), taps] = top
            part_copy(a, step).start()

    groups = tm // line

    def more_copy(a, step):
        at = a * groups + step
        spot = lax.rem(outer + step, groups)
        return remote(
            more.at[a, outer], more.at[a, outer], more_send.at[at], more_recv.at[at],
            device(tm=spot * line + inner),
        )

    def line_copy(a, step):
        at = a * line + step
        block = full.at[a, mine, inner]
        return remote(
            block, block, line_send.at[at], line_recv.at[at],
            device(tm=outer * line + along(step)),
        )

    def collect(a):
        value = total[a, inner]
        for step in range(1, line):
            part_copy(a, step).wait()
        for step in range(1, line):
            value = value + decode(land[a, along(step)], taps)
        if groups > 1:
            value, top = encode(value)
            more[a, outer, pl.ds(0, taps)] = value
            more[a, outer, taps] = top
            for step in range(1, groups):
                more_copy(a, step).start()
            for step in range(1, groups):
                more_copy(a, step).wait()
            value = decode(more[a, 0], taps)
            for k in range(1, groups):
                value = value + decode(more[a, k], taps)
        value, top = encode(value)
        full[a, mine, inner, pl.ds(0, taps)] = value
        full[a, mine, inner, taps] = top
        for step in range(1, line):
            line_copy(a, step).start()

    half = line // 2
    sides = [("rows", s) for s in range(1, near)] + [("dp", i) for i in range(1, dp)]

    def go(side):
        axis, step = side
        return {axis: shift(axis, step * (pair if axis == "rows" else 1))}

    def come(side):
        axis, step = side
        return {axis: shift(axis, -step * (pair if axis == "rows" else 1))}

    def number(place):
        place = dict(me, **place)
        return place["dp"] * rows + place["rows"]

    def near_copy(a, side):
        at = a * len(sides) + sides.index(side)
        block = full.at[a, mine]
        return remote(block, block, near_send.at[at], near_recv.at[at], device(**go(side)))

    turns = []
    for one in sides:
        for two in sides:
            if one[0] == two[0]:
                continue
            rest = (0, half) if one[0] == "rows" else (half, line - half)
            if rest[1]:
                turns.append((one, two, rest))

    def turn_copy(a, turn):
        one, two, rest = turn
        at = a * len(turns) + turns.index(turn)
        block = full.at[a, number(come(one)), pl.ds(*rest)]
        return remote(block, block, turn_send.at[at], turn_recv.at[at], device(**go(two)))

    hops = [(None, None)] + [(side, None) for side in sides] + turns

    def pair_copy(a, k):
        at = a * len(hops) + k
        if k == 0:
            block = full.at[a, mine]
        elif k <= len(sides):
            block = full.at[a, number(come(hops[k][0]))]
        else:
            one, two, rest = hops[k]
            block = full.at[a, number(dict(come(one), **come(two))), pl.ds(*rest)]
        return remote(block, block, pair_send.at[at], pair_recv.at[at], device(rows=partner))

    def spread(a):
        for step in range(1, line):
            line_copy(a, step).wait()
        for side in sides:
            near_copy(a, side).start()
        if pair == 2:
            pair_copy(a, 0).start()

    def relay(a):
        for k, side in enumerate(sides):
            near_copy(a, side).wait()
            for turn in turns:
                if turn[0] == side:
                    turn_copy(a, turn).start()
            if pair == 2:
                pair_copy(a, 1 + k).start()

    def handover(a):
        for k, turn in enumerate(turns):
            turn_copy(a, turn).wait()
            if pair == 2:
                pair_copy(a, 1 + len(sides) + k).start()

    def finish(a):
        if pair == 2:
            for k in range(len(hops)):
                pair_copy(a, k).wait()
        per = LANES // part

        def tap(k, carry):
            for high in range(chans // LANES):
                for low in range(chans // LANES):
                    at = low * LANES
                    pile = []
                    for n in range(high * per, (high + 1) * per):
                        block = full.at[a, n // line, n % line]
                        unit = block[taps, :, at : at + LANES].astype(jnp.float32)
                        value = jnp.log(block[k, :, at : at + LANES].astype(jnp.float32))
                        pile.append(value * (unit * (1.0 / (SPAN * math.log(2.0)))))
                    out_ref[a * taps + k, at : at + LANES, high * LANES : (high + 1) * LANES] = (
                        jnp.concatenate(pile, axis=0).T
                    )
            return carry

        lax.fori_loop(0, taps, tap, 0)

    def end_copy(step):
        return remote(
            small_mine, small_line.at[me["tm"]], end_send.at[step], end_recv.at[step],
            device(tm=shift("tm", step)),
        )

    def small_middle():
        for i, s in pieces[1:]:
            sum_copy(i, s).wait()
        small_mine[...] = jnp.sum(small_plane[...], axis=0)
        small_line[me["tm"]] = small_mine[...]
        for step in range(1, tm):
            end_copy(step).start()

    def small_end():
        for step in range(1, tm):
            end_copy(step).wait()
        value = jnp.sum(small_line[...], axis=0)
        bias_out[...] = value[0:1]
        head_out[...] = value[1:2]

    stages = (scatter, collect, spread, relay, handover, finish)
    for wave in range(len(stages) + TAPS - 1):
        for a in range(TAPS):
            level = wave - a
            if 0 <= level < len(stages):
                stages[level](a)
        if wave == 0:
            small_middle()
        if wave == 3:
            small_end()


def per_device(sizes, clips, weight, bias, head):
    dp, tm, rows = sizes
    _, frames, _, cols, chans = clips.shape
    count = frames * cols
    plane = dp * rows
    share = chans // plane
    line, groups = split_line(tm, share // SUB)
    part = share // line
    taps = TAPS**2
    pair = 2 if rows % 2 == 0 else 1
    near = rows // pair
    close = dp * near - 1
    sides = near - 1 + dp - 1
    turns = 2 * (near - 1) * (dp - 1)
    pad = pltpu.VMEM((frames + 2, 3, cols, chans), jnp.bfloat16)
    field = pltpu.VMEM((count, chans), jnp.float32)
    gathered = pltpu.VMEM((plane, count, chans), jnp.bfloat16)
    coded = pltpu.VMEM((TAPS, line, taps + 1, part, chans), jnp.bfloat16)

    def dma(n):
        return pltpu.SemaphoreType.DMA((max(n, 1),))

    sems = []
    for n in (
        24, 2 * close, 2 * (close + 1), 6 * plane, TAPS * line, TAPS * groups,
        TAPS * line, TAPS * sides, TAPS * turns, TAPS * (1 + sides + turns), plane, tm,
    ):
        sems += [dma(n), dma(n)]
    vmem = pl.BlockSpec(memory_space=pltpu.VMEM)
    hbm = pl.BlockSpec(memory_space=pl.ANY)
    grad_weight, grad_bias, grad_head = pl.pallas_call(
        functools.partial(kernel, sizes, line),
        out_shape=(
            pltpu.VMEM((TAPS**3, chans, chans), jnp.float32),
            pltpu.VMEM((1, chans), jnp.float32),
            pltpu.VMEM((1, chans), jnp.float32),
        ),
        in_specs=[hbm, hbm, vmem, vmem],
        out_specs=(vmem, vmem, vmem),
        scratch_shapes=[
            pltpu.VMEM((TAPS**3, chans, chans), jnp.bfloat16),
            pad, pad, pad,
            pltpu.VMEM((TAPS, count, chans), jnp.float32),
            field, field,
            gathered, gathered,
            pltpu.VMEM((2, frames, chans, cols), jnp.bfloat16),
            pltpu.VMEM((2, plane, frames + 2, share, cols), jnp.bfloat16),
            pltpu.VMEM((2, dp, rows + 2, frames + 2, TAPS * share, cols), jnp.bfloat16),
            pltpu.VMEM((TAPS, taps * share, chans), jnp.float32),
            pltpu.VMEM((TAPS, line, taps, part, chans), jnp.float32),
            coded, coded,
            pltpu.VMEM((TAPS, groups, taps + 1, part, chans), jnp.bfloat16),
            pltpu.VMEM((TAPS, plane, line, taps + 1, part, chans), jnp.bfloat16),
            pltpu.VMEM((SUB, chans), jnp.float32),
            pltpu.VMEM((plane, SUB, chans), jnp.float32),
            pltpu.VMEM((tm, SUB, chans), jnp.float32),
            dma(2), *sems,
        ],
        compiler_params=pltpu.CompilerParams(
            collective_id=0, has_side_effects=True, vmem_limit_bytes=48 * 1024 * 1024
        ),
    )(
        pltpu.with_memory_space_constraint(clips.reshape(frames, cols, chans), pltpu.HBM),
        weight.reshape(TAPS**3, chans, chans),
        bias.reshape(1, chans),
        head.reshape(1, chans),
    )
    grad_weight = grad_weight.reshape(TAPS, TAPS, TAPS, chans, chans)
    return grad_weight, grad_bias.reshape(chans), grad_head.reshape(chans)


def solution(mesh):
    sizes = tuple(mesh.shape[axis] for axis in ("dp", "tm", "rows"))
    return jax.shard_map(
        functools.partial(per_device, sizes),
        mesh=mesh,
        in_specs=(P("dp", "tm", "rows", None, None), P(), P(), P()),
        out_specs=(P(), P(), P()),
        check_vma=False,
    )
```

time: 86.5 us -> 82.9 us (0.958)
  Pallas kernels: 85.6 us -> 78 us
  local copies, waits for them, and re-layouts: 0 us -> 4.09 us
    pallas_call x2 -> x1, Pallas kernels: 85.6 us -> 78 us  [per_device(): pl.pallas_call(functools.partial(kernel, sizes, line), out_shape=(pltpu.V...]
    unnamed x0 -> x3, local copies, waits for them, and re-layouts: none -> 4.09 us
where the time goes in v1:
time: 82.9 us; the launch traced here: 82.8 us
  Pallas kernels  78 us (94%)
  local copies, waits for them, and re-layouts  4.09 us (5%)
    pallas_call x1, Pallas kernels, per_device(): pl.pallas_call(functools.partial(kernel, sizes, line), out_shape=(pltpu.V...  78 us
    unnamed x3, local copies, waits for them, and re-layouts  4.09 us

profile of v1, /device:TPU:0, one launch (start us, length us, event | category | flops | bytes accessed | tf_op | source)
XLA Modules:
  0.0 82.8 jit_solution(7660468995361205452)
XLA Ops:
  0.6 78.0 %shard_map.67 = (f32[27,256,256]{2,1,0:T(8,128)S(1)}, f32[1,256]{1,0:T(1,128)S(1)}, f32[1,256]{1,0:T(1,128)S(1)}) custom-call(bf16[2,128,256]{2,1,0:T(8,128)(2,1)} %bitcast.11, bf16[27,256,256]{2,1,0:T(8,128)(2,1)} %bitcast.10, f32[1,256]{1,0:T(1,128)} %bitcast.12, f32[1,256]{1,0:T(1,128)} %bitcast.13), custom_call_target="tpu_custom_call" | custom-call | tf_op jit(solution)/shard_map/pallas_call | solution.py:567
  78.7 3.0 %copy.10 = f32[3,3,3,256,256]{4,3,2,1,0:T(8,128)} copy(f32[3,3,3,256,256]{4,3,2,1,0:T(8,128)S(1)} %bitcast.7) | data formatting | bytes 14155776
  81.6 0.6 copy.11
  82.2 0.6 copy.12

commit v2 on v1

v2 whole, which is shorter than its diff:
```python
import functools
import math

import jax
import jax.numpy as jnp
from jax import lax
from jax.experimental import pallas as pl
from jax.experimental.pallas import tpu as pltpu
from jax.sharding import PartitionSpec as P

penalty_weight = 0.01
MESH = pl.DeviceIdType.MESH
SUB = 8
TAPS = 3
SPAN = 120.0
LANES = 128
WIDE = 128


def split_line(tm, most):
    line = 1
    while tm % (2 * line) == 0 and 2 * line <= most:
        line *= 2
    return line, tm // line


def decode(block, taps):
    unit = block[taps].astype(jnp.float32) * (1.0 / (SPAN * math.log(2.0)))
    return jnp.log(block[:taps].astype(jnp.float32)) * unit[None]


def encode(value):
    top = (jnp.max(jnp.abs(value), axis=0) * 1.01 + 1e-30).astype(jnp.bfloat16)
    rate = SPAN / top.astype(jnp.float32)
    return jnp.exp2(value * rate[None]).astype(jnp.bfloat16), top


def kernel(
    sizes, line, clips_ref, weight_ref, bias_ref, head_ref,
    out_ref, bias_out, head_out,
    w_ref, wt_ref, clip_pad, score_pad, grad_pad, acc, slope_ref, curve_ref,
    clip_all, grad_all, turned, slices, shifts, first, total, code, land, more, full,
    small_mine, small_plane, small_line,
    local_sem, halo_send, halo_recv, hand_send, hand_recv, all_send, all_recv, pass_send, pass_recv,
    slice_send, slice_recv, part_send, part_recv, more_send, more_recv,
    line_send, line_recv, near_send, near_recv, turn_send, turn_recv, pair_send, pair_recv,
    sum_send, sum_recv, end_send, end_recv,
):
    dp, tm, rows = sizes
    frames, cols, chans = clips_ref.shape
    count = frames * cols
    plane = dp * rows
    share = chans // plane
    part = share // line
    taps = TAPS**2
    pair = 2 if rows % 2 == 0 else 1
    near = rows // pair
    me = {"dp": lax.axis_index("dp"), "tm": lax.axis_index("tm"), "rows": lax.axis_index("rows")}
    mine = me["dp"] * rows + me["rows"]

    def device(**moved):
        place = dict(me, **moved)
        return (place["dp"], place["tm"], place["rows"])

    def shift(axis, step):
        return lax.rem(me[axis] + step % dict(dp=dp, tm=tm, rows=rows)[axis], dict(dp=dp, tm=tm, rows=rows)[axis])

    def remote(src, dst, send, recv, target):
        return pltpu.make_async_remote_copy(
            src_ref=src, dst_ref=dst, send_sem=send, recv_sem=recv,
            device_id=target, device_id_type=MESH,
        )

    weight_copy = pltpu.make_async_copy(weight_ref, w_ref, local_sem.at[0])
    weight_copy.start()
    clip_copy = pltpu.make_async_copy(
        clips_ref, clip_pad.at[pl.ds(1, frames), 1], local_sem.at[1]
    )
    clip_copy.start()
    keep_copy = pltpu.make_async_copy(clips_ref, clip_all.at[mine], local_sem.at[2])
    keep_copy.start()

    steps = {(i, t % tm, s) for i in range(dp) for t in (-1, 0, 1) for s in range(rows)}
    steps |= {(0, t, 0) for t in range(tm)}
    steps = sorted(steps - {(0, 0, 0)})
    barrier = pltpu.get_barrier_semaphore()
    for i, t, s in steps:
        pl.semaphore_signal(
            barrier, inc=1, device_id=(shift("dp", i), shift("tm", t), shift("rows", s)),
            device_id_type=MESH,
        )
    for axis, bound, fill in (
        ("rows", 0, lambda pad: pad.at[:, 0]), ("rows", rows - 1, lambda pad: pad.at[:, 2]),
        ("tm", 0, lambda pad: pad.at[0]), ("tm", tm - 1, lambda pad: pad.at[frames + 1]),
    ):
        @pl.when(me[axis] == bound)
        def _():
            for pad in (clip_pad, score_pad, grad_pad):
                at = fill(pad)
                at[...] = jnp.zeros(at.shape, at.dtype)
    for which in range(2):
        for edge in (0, rows + 1):
            shifts[which, :, edge] = jnp.zeros(shifts.shape[1:2] + shifts.shape[3:], shifts.dtype)
        for edge, bound in ((0, 0), (frames + 1, tm - 1)):
            @pl.when(me["tm"] == bound)
            def _():
                slices[which, :, edge] = jnp.zeros((plane, share, cols), slices.dtype)
    pl.semaphore_wait(barrier, len(steps))

    moves = [(t, r) for t in (-1, 0, 1) for r in (-1, 0, 1) if (t, r) != (0, 0)]
    partner = me["rows"] + 1 - 2 * lax.rem(me["rows"], 2) if pair == 2 else me["rows"]
    mirror = rows - 1 - me["rows"]
    toward = partner - me["rows"]

    def inside(t, r):
        ok = None
        for axis, step, size in (("tm", t, tm), ("rows", r, rows)):
            if step:
                cond = me[axis] > 0 if step < 0 else me[axis] < size - 1
                ok = cond if ok is None else jnp.logical_and(ok, cond)
        return ok

    def leaves(t, r, sender):
        ok = inside(t, r) if sender else inside(-t, -r)
        if pair == 1:
            return ok
        row = me["rows"] if sender else me["rows"] - r
        return jnp.logical_and(ok, lax.rem(row, 2) == (0 if r < 0 else 1))

    def halo_copy(which, pad, source, t, r):
        slot = which * len(moves) + moves.index((t, r))
        if t == 0:
            here, there = pl.ds(0, frames), pl.ds(1, frames)
        elif t > 0:
            here, there = pl.ds(frames - 1, 1), pl.ds(0, 1)
        else:
            here, there = pl.ds(0, 1), pl.ds(frames + 1, 1)
        return remote(
            source.at[here], pad.at[there, 1 - r], halo_send.at[slot], halo_recv.at[slot],
            device(tm=me["tm"] + t, rows=me["rows"] + r),
        )

    def hand_copy(which, pad, t):
        at = 2 * which + (t > 0)
        edge = 0 if t > 0 else frames + 1
        return remote(
            pad.at[edge, 1], pad.at[edge, 1 - toward], hand_send.at[at], hand_recv.at[at],
            device(rows=partner),
        )

    def depth_start(which, pad, source):
        for t in (-1, 1):
            @pl.when(inside(t, 0))
            def _():
                halo_copy(which, pad, source, t, 0).start()

    def side_start(which, pad, source):
        for r in (-1, 1):
            @pl.when(inside(0, r))
            def _():
                halo_copy(which, pad, source, 0, r).start()

    def corner_start(which, pad, source):
        for t in (-1, 1):
            for r in (-1, 1):
                @pl.when(leaves(t, r, True))
                def _():
                    halo_copy(which, pad, source, t, r).start()

    def side_sent(which, pad, source):
        for r in (-1, 1):
            @pl.when(inside(0, r))
            def _():
                halo_copy(which, pad, source, 0, r).wait_send()

    def side_wait(which, pad, source):
        for r in (-1, 1):
            @pl.when(inside(0, -r))
            def _():
                halo_copy(which, pad, source, 0, r).wait_recv()

    def depth_wait(which, pad, source):
        for t in (-1, 1):
            @pl.when(inside(-t, 0))
            def _():
                halo_copy(which, pad, source, t, 0).wait_recv()
                if pair == 2:
                    hand_copy(which, pad, t).start()
        for t in (-1, 1):
            @pl.when(inside(t, 0))
            def _():
                halo_copy(which, pad, source, t, 0).wait_send()

    def corner_wait(which, pad, source):
        for t in (-1, 1):
            for r in (-1, 1):
                @pl.when(leaves(t, r, True))
                def _():
                    halo_copy(which, pad, source, t, r).wait_send()

                @pl.when(leaves(t, r, False))
                def _():
                    halo_copy(which, pad, source, t, r).wait_recv()
            if pair == 2:
                @pl.when(inside(-t, 0))
                def _():
                    hand_copy(which, pad, t).wait()

    column = lax.rem(lax.broadcasted_iota(jnp.int32, (count, chans), 0), cols)

    def earlier(value):
        return jnp.where(column == 0, 0.0, pltpu.roll(value, 1, 0))

    def later(value):
        return jnp.where(column == cols - 1, 0.0, pltpu.roll(value, count - 1, 0))

    def conv(which, pad, source, kernel_ref, idle, sent, side, between):
        def put(shift_f, start, many, places, new=False):
            if not many:
                return
            left = jnp.concatenate(
                [
                    pad[pl.ds(start + shift_f, many), b].reshape(many * cols, chans)
                    for b in places
                ],
                axis=1,
            )
            at = pl.ds(start * cols, many * cols)
            for d in range(TAPS):
                taps = [kernel_ref[(shift_f * TAPS + b) * TAPS + d] for b in places]
                value = jnp.dot(
                    left, jnp.concatenate(taps, axis=0), preferred_element_type=jnp.float32
                )
                acc[d, at] = value if new else acc[d, at] + value

        def inner_frames(places, new):
            put(1, 0, frames, places, new)
            put(0, 1, frames - 1, places)
            put(2, 0, frames - 1, places)

        def outer_frames(places):
            put(0, 0, 1, places)
            put(2, frames - 1, 1, places)

        inner_frames((1,), True)
        corner_start(which, pad, source)
        idle()
        side(which, pad, source)
        inner_frames((0, 2), False)
        depth_wait(which, pad, source)
        between()
        outer_frames((1,))
        corner_wait(which, pad, source)
        outer_frames((0, 2))
        sent()
        return earlier(acc[0]) + acc[1] + later(acc[2])

    others = range(1, dp)
    across = [(0, 0)] + [(i, 0) for i in others]
    if near == 2:
        across = [(0, 0), (0, 1)] + [(i, 0) for i in others] + [(i, 1) for i in others]

    edge = jnp.logical_and(me["rows"] > 0, me["rows"] < rows - 1)

    def spot(i, m):
        return shift("dp", -i) * rows + (mirror if m else me["rows"])

    def all_copy(which, buf, i, m):
        at = which * len(across) + across.index((i, m))
        if i == 0:
            block, there = buf.at[mine], device(rows=mirror)
        else:
            block, there = buf.at[spot(0, m)], device(dp=shift("dp", i))
        return remote(block, block, all_send.at[at], all_recv.at[at], there)

    def pass_copy(which, buf, i, m):
        at = which * len(across) + across.index((i, m))
        block = buf.at[spot(i, m)]
        return remote(block, block, pass_send.at[at], pass_recv.at[at], device(rows=partner))

    def all_start(which, buf):
        if pair == 2:
            pass_copy(which, buf, 0, 0).start()
        if near == 2:
            @pl.when(edge)
            def _():
                all_copy(which, buf, 0, 1).start()

    def all_down(which, buf):
        for i in others:
            all_copy(which, buf, i, 0).start()

    def all_side(buf):
        def side(which, pad, source):
            at = which // 2
            if pair == 2:
                pass_copy(at, buf, 0, 0).wait_recv()
                pad[pl.ds(1, frames), 1 + toward] = buf[me["dp"] * rows + partner]
            if near == 2:
                @pl.when(edge)
                def _():
                    all_copy(at, buf, 0, 1).wait_recv()
                    pad[pl.ds(1, frames), 1 - toward] = buf[me["dp"] * rows + mirror]

        return side

    def all_sent(which, buf):
        if near == 2:
            @pl.when(edge)
            def _():
                all_copy(which, buf, 0, 1).wait_send()

    def relay_start(which, buf):
        for i in others:
            all_copy(which, buf, i, 1).start()
        pass_copy(which, buf, 0, 1).start()

    def all_between(which, buf):
        if near == 2:
            @pl.when(edge)
            def _():
                relay_start(which, buf)

            @pl.when(jnp.logical_not(edge))
            def _():
                all_copy(which, buf, 0, 1).start()

    def all_relay(which, buf):
        if near == 2:
            @pl.when(jnp.logical_not(edge))
            def _():
                all_copy(which, buf, 0, 1).wait_recv()
                relay_start(which, buf)

    def all_near(which, buf):
        if near == 2:
            pass_copy(which, buf, 0, 1).wait_recv()

    def all_far(which, buf, m):
        if m and near != 2:
            return
        for i in others:
            all_copy(which, buf, i, m).wait_recv()
            if pair == 2:
                pass_copy(which, buf, i, m).start()

    def all_end(which, buf):
        for i, m in across:
            if (i, m) == (0, 1):
                @pl.when(jnp.logical_not(edge))
                def _():
                    all_copy(which, buf, i, m).wait_send()
            elif i:
                all_copy(which, buf, i, m).wait_send()
            if pair == 2:
                pass_copy(which, buf, i, m).wait_send()
                if i:
                    pass_copy(which, buf, i, m).wait_recv()

    def slice_copy(which, t, i, s):
        at = which * 3 + t + 1
        y, r = shift("dp", i), shift("rows", s)
        rest = pl.ds(pl.multiple_of((y * rows + r) * share, share), share)
        if t == 0:
            src, dst = turned.at[which, :, rest], slices.at[which, mine, pl.ds(1, frames)]
        elif t > 0:
            src, dst = turned.at[which, frames - 1, rest], slices.at[which, mine, 0]
        else:
            src, dst = turned.at[which, 0, rest], slices.at[which, mine, frames + 1]
        return remote(
            src, dst, slice_send.at[at], slice_recv.at[at],
            device(dp=y, rows=r, tm=me["tm"] + t),
        )

    pieces = [(i, s) for i in range(dp) for s in range(rows)]

    def slice_start(which, value):
        for f in range(frames):
            turned[which, f] = value[f].T.astype(jnp.bfloat16)
        for t in (1, -1):
            @pl.when(inside(t, 0))
            def _():
                for i, s in pieces:
                    slice_copy(which, t, i, s).start()
        for i, s in pieces[1:]:
            slice_copy(which, 0, i, s).start()
        own = pl.ds(pl.multiple_of(mine * share, share), share)
        for f in range(frames):
            slices[which, mine, f + 1] = turned[which, f, own]

    lane = lax.broadcasted_iota(jnp.int32, (share, cols), 1)

    def slice_end(which):
        def whole(t):
            at = which * 3 + t + 1
            block = slices.at[which, :, 0] if t else slices.at[
                which, pl.ds(0, plane - 1), pl.ds(1, frames)
            ]
            return remote(block, block, slice_send.at[at], slice_recv.at[at], device())

        for t in (1, -1):
            @pl.when(inside(t, 0))
            def _():
                whole(t).wait_send()

            @pl.when(inside(-t, 0))
            def _():
                whole(t).wait_recv()
        whole(0).wait()
        for j in range(plane):
            for f in range(frames + 2):
                value = slices[which, j, f].astype(jnp.float32)
                after = jnp.where(lane == cols - 1, 0.0, pltpu.roll(value, cols - 1, 1))
                before = jnp.where(lane == 0, 0.0, pltpu.roll(value, 1, 1))
                shifts[which, j // rows, j % rows + 1, f] = jnp.concatenate(
                    [after, value, before], axis=0
                ).astype(jnp.bfloat16)

    def correlate(which, buf, a, clips):
        left = jnp.concatenate(
            [
                jnp.concatenate(
                    [
                        shifts[which, y, r + 2 - b, f + 2 - a]
                        for y in clips for r in range(rows) for f in range(frames)
                    ],
                    axis=1,
                )
                for b in range(TAPS)
            ],
            axis=0,
        )
        right = jnp.concatenate(
            [buf[pl.ds(y * rows, rows)].reshape(rows * count, chans) for y in clips], axis=0
        )
        return jnp.dot(left, right, preferred_element_type=jnp.float32)

    def turn_weight():
        def one(k, carry):
            wt_ref[TAPS**3 - 1 - k] = w_ref[k].T
            return carry

        lax.fori_loop(0, TAPS**3, one, 0, unroll=3)

    depth_start(0, clip_pad, clips_ref)
    clip_copy.wait()
    keep_copy.wait()
    all_start(0, clip_all)
    all_down(0, clip_all)
    weight_copy.wait()
    pre = bias_ref[...] + conv(
        0, clip_pad, clips_ref, w_ref, turn_weight, lambda: all_sent(0, clip_all),
        all_side(clip_all), lambda: all_between(0, clip_all),
    )
    sig = jax.nn.sigmoid(pre)
    slope = sig * (1.0 + pre * (1.0 - sig))
    slope_ref[...] = slope
    curve_ref[...] = sig * (1.0 - sig) * (2.0 + pre * (1.0 - 2.0 * sig))
    score = (head_ref[...] * slope).astype(jnp.bfloat16)
    score_pad[pl.ds(1, frames), 1] = score.reshape(frames, cols, chans)
    score_own = score_pad.at[pl.ds(1, frames), 1]
    depth_start(1, score_pad, score_own)
    side_start(1, score_pad, score_own)
    all_relay(0, clip_all)
    all_far(0, clip_all, 0)

    input_grad = conv(
        1, score_pad, score_own, wt_ref, lambda: None,
        lambda: side_sent(1, score_pad, score_own), side_wait,
        lambda: slice_start(0, score_pad[pl.ds(1, frames), 1].astype(jnp.float32)),
    ).astype(jnp.bfloat16).reshape(frames, cols, chans)
    grad_pad[pl.ds(1, frames), 1] = input_grad
    grad_all[mine] = input_grad
    grad_own = grad_pad.at[pl.ds(1, frames), 1]
    depth_start(2, grad_pad, grad_own)
    all_start(1, grad_all)
    all_down(1, grad_all)
    all_far(0, clip_all, 1)

    back = penalty_weight * conv(
        2, grad_pad, grad_own, w_ref, lambda: None, lambda: all_sent(1, grad_all),
        all_side(grad_all), lambda: all_between(1, grad_all),
    )
    pre_grad = back * head_ref[...] * curve_ref[...]
    slice_start(
        1, pre_grad.astype(jnp.bfloat16).astype(jnp.float32).reshape(frames, cols, chans)
    )
    small_mine[...] = jnp.zeros_like(small_mine)
    small_mine[pl.ds(0, 1)] = jnp.sum(pre_grad, axis=0, keepdims=True)
    small_mine[pl.ds(1, 1)] = jnp.sum(back * slope_ref[...], axis=0, keepdims=True)

    def sum_copy(i, s):
        return remote(
            small_mine, small_plane.at[mine], sum_send.at[0], sum_recv.at[0],
            device(dp=shift("dp", i), rows=shift("rows", s)),
        )

    small_plane[mine] = small_mine[...]
    for i, s in pieces[1:]:
        sum_copy(i, s).start()

    slice_end(0)
    all_relay(1, grad_all)
    all_far(1, grad_all, 0)
    all_near(0, clip_all)
    all_end(0, clip_all)
    all_near(1, grad_all)
    for a in range(TAPS):
        first[a] = correlate(0, grad_all, a, [me["dp"]])
    all_far(1, grad_all, 1)
    all_end(1, grad_all)
    for a in range(TAPS):
        first[a] = penalty_weight * (
            first[a] + correlate(0, grad_all, a, [shift("dp", i) for i in others])
            if dp > 1 else first[a]
        )

    slice_end(1)
    inner, outer = lax.rem(me["tm"], line), me["tm"] // line
    wide = full.shape[-1]
    chunks = [(a, low) for a in range(TAPS) for low in range(chans // wide)]

    def along(step):
        return lax.rem(inner + step, line)

    def part_copy(c, step):
        return remote(
            code.at[c, along(step)], land.at[c, inner], part_send.at[c], part_recv.at[c],
            device(tm=outer * line + along(step)),
        )

    def part_all(c):
        block = land.at[c, pl.ds(0, line - 1)]
        return remote(block, block, part_send.at[c], part_recv.at[c], device())

    def scatter(c):
        a, low = chunks[c]
        if low == 0:
            both = (first[a] + correlate(1, clip_all, a, range(dp))).reshape(taps, share, chans)
            for k in range(chans // wide):
                for t in range(line):
                    total[c + k, t] = both[
                        :, t * part : (t + 1) * part, k * wide : (k + 1) * wide
                    ]
        for step in range(line - 1, 0, -1):
            value, top = encode(total[c, along(step)])
            code[c, along(step), pl.ds(0, taps)] = value
            code[c, along(step), taps] = top
        if c > 1 and line > 1:
            part_all(c - 2).wait_send()
        for step in range(line - 1, 0, -1):
            part_copy(c, step).start()

    groups = tm // line

    def more_copy(c, step):
        spot = lax.rem(outer + step, groups)
        return remote(
            more.at[c, outer], more.at[c, outer], more_send.at[c], more_recv.at[c],
            device(tm=spot * line + inner),
        )

    upper = inner // 2
    ranks = [inner, inner + 1 - 2 * lax.rem(inner, 2), 2 - upper, 3 - 3 * upper][:line]
    middle = lax.rem(inner + upper, 2) == 1

    def line_copy(c, rank, to):
        here = full.at[c, mine * line + ranks[rank]]
        return remote(
            here, here, line_send.at[c], line_recv.at[c * line + ranks[rank]],
            device(tm=outer * line + to),
        )

    def collect(c):
        value = total[c, inner]
        if line > 1:
            part_all(c).wait_recv()
            if c >= len(chunks) - 2:
                part_all(c).wait_send()
        for step in range(1, line):
            value = value + decode(land[c, along(step)], taps)
        if groups > 1:
            value, top = encode(value)
            more[c, outer, pl.ds(0, taps)] = value
            more[c, outer, taps] = top
            for step in range(1, groups):
                more_copy(c, step).start()
            block = more.at[c, pl.ds(0, groups - 1)]
            remote(block, block, more_send.at[c], more_recv.at[c], device()).wait()
            value = decode(more[c, 0], taps)
            for k in range(1, groups):
                value = value + decode(more[c, k], taps)
        value, top = encode(value)
        full[c, mine * line + inner, pl.ds(0, taps)] = value
        full[c, mine * line + inner, taps] = top
        for rank in range(min(line - 1, 2), 0, -1):
            line_copy(c, 0, ranks[rank]).start()
        share_out(c, 0)

    def share_out(c, rank):
        for side in sides:
            near_copy(c, rank, side).start()
        if pair == 2:
            pair_copy(c, rank, 0).start()

    def take(c, rank):
        line_copy(c, rank, inner).wait_recv()
        if rank > 1:
            @pl.when(middle)
            def _():
                line_copy(c, rank, ranks[1]).start()
        share_out(c, rank)

    sides = [("rows", s) for s in range(1, near)] + [("dp", i) for i in range(1, dp)]

    def go(side):
        axis, step = side
        return {axis: shift(axis, step * (pair if axis == "rows" else 1))}

    def come(side):
        axis, step = side
        return {axis: shift(axis, -step * (pair if axis == "rows" else 1))}

    def number(place):
        place = dict(me, **place)
        return place["dp"] * rows + place["rows"]

    turns = [(one, two) for one in sides for two in sides if one[0] != two[0]]
    hops = [()] + [(side,) for side in sides] + turns

    def block_at(c, rank, hop):
        place = {}
        for side in hop:
            place.update(come(side))
        return full.at[c, number(place) * line + ranks[rank]]

    def turned_by(rank):
        return [turn for turn in turns if turn[0][0] == ("dp" if rank % 2 else "rows")]

    per_turn = max(1, len(turns) // 2)

    def near_copy(c, rank, side):
        at = (c * line + rank) * len(sides) + sides.index(side)
        block = block_at(c, rank, ())
        return remote(block, block, near_send.at[c], near_recv.at[at], device(**go(side)))

    def turn_copy(c, rank, turn):
        at = (c * line + rank) * per_turn + turned_by(rank).index(turn)
        block = block_at(c, rank, turn[:1])
        return remote(block, block, turn_send.at[c], turn_recv.at[at], device(**go(turn[1])))

    def pair_copy(c, rank, k):
        block = block_at(c, rank, hops[k])
        return remote(block, block, pair_send.at[c], pair_recv.at[c], device(rows=partner))

    def relay(c, rank):
        for k, side in enumerate(sides):
            near_copy(c, rank, side).wait_recv()
            for turn in turned_by(rank):
                if turn[0] == side:
                    turn_copy(c, rank, turn).start()
            if pair == 2:
                pair_copy(c, rank, 1 + k).start()

    def handover(c, rank):
        for turn in turned_by(rank):
            turn_copy(c, rank, turn).wait_recv()
            if pair == 2:
                pair_copy(c, rank, hops.index(turn)).start()

    def finish(c):
        a, low = chunks[c]
        ended = [(near_send, line * len(sides)), (turn_send, sum(len(turned_by(k)) for k in range(line)))]
        for sem, n in ended + [(line_send, min(line - 1, 2))]:
            if n:
                block = full.at[c, pl.ds(0, n)]
                remote(block, block, sem.at[c], sem.at[c], device()).wait_send()
        if line == 4:
            @pl.when(middle)
            def _():
                block = full.at[c, pl.ds(0, 2)]
                remote(block, block, line_send.at[c], line_send.at[c], device()).wait_send()
        if pair == 2:
            block = full.at[c, pl.ds(0, plane * line // 2)]
            remote(block, block, pair_send.at[c], pair_recv.at[c], device()).wait()
        per = LANES // part

        def tap(k, carry):
            for high in range(chans // LANES):
                for left in range(0, wide, LANES):
                    pile = []
                    for n in range(high * per, (high + 1) * per):
                        block = full.at[c, n]
                        unit = block[taps, :, left : left + LANES].astype(jnp.float32)
                        value = jnp.log(block[k, :, left : left + LANES].astype(jnp.float32))
                        pile.append(value * (unit * (1.0 / (SPAN * math.log(2.0)))))
                    out_ref[
                        a * taps + k, low * wide + left : low * wide + left + LANES,
                        high * LANES : (high + 1) * LANES,
                    ] = jnp.concatenate(pile, axis=0).T
            return carry

        lax.fori_loop(0, taps, tap, 0, unroll=True)

    def end_copy(step):
        return remote(
            small_mine, small_line.at[me["tm"]], end_send.at[0], end_recv.at[0],
            device(tm=shift("tm", step)),
        )

    def small_middle():
        block = small_plane.at[pl.ds(0, plane - 1)]
        if plane > 1:
            remote(block, block, sum_send.at[0], sum_recv.at[0], device()).wait()
        small_mine[...] = jnp.sum(small_plane[...], axis=0)
        small_line[me["tm"]] = small_mine[...]
        for step in range(1, tm):
            end_copy(step).start()

    def small_end():
        block = small_line.at[pl.ds(0, tm - 1)]
        if tm > 1:
            remote(block, block, end_send.at[0], end_recv.at[0], device()).wait()
        value = jnp.sum(small_line[...], axis=0)
        bias_out[...] = value[0:1]
        head_out[...] = value[1:2]

    pace = 1.77 * wide / LANES
    order = [(4.0, small_middle, ()), (16.0, small_end, ())]
    for c in range(len(chunks)):
        got = 2.9 + pace + pace * c
        order += [(pace * max(c - 1, 0), scatter, (c,)), (got, collect, (c,))]
        for rank in range(line):
            here = got + (0.0, 3.5, 5.0, 6.5)[rank]
            if rank:
                order.append((here, take, (c, rank)))
            order += [(here + 3.5, relay, (c, rank)), (here + 7.5, handover, (c, rank))]
        order.append((got + 16.5, finish, (c,)))
    for _, stage, what in sorted(order, key=lambda entry: entry[0]):
        stage(*what)


def per_device(sizes, clips, weight, bias, head):
    dp, tm, rows = sizes
    _, frames, _, cols, chans = clips.shape
    count = frames * cols
    plane = dp * rows
    share = chans // plane
    line, groups = split_line(tm, share // SUB)
    part = share // line
    taps = TAPS**2
    pair = 2 if rows % 2 == 0 else 1
    near = rows // pair
    if rows not in (1, 2, 4):
        raise ValueError("rows")
    sides = near - 1 + dp - 1
    turns = 2 * (near - 1) * (dp - 1)
    pad = pltpu.VMEM((frames + 2, 3, cols, chans), jnp.bfloat16)
    field = pltpu.VMEM((count, chans), jnp.float32)
    gathered = pltpu.VMEM((plane, frames, cols, chans), jnp.bfloat16)
    wide = WIDE if chans % WIDE == 0 else chans
    chunks = TAPS * (chans // wide)
    coded = pltpu.VMEM((chunks, line, taps + 1, part, wide), jnp.bfloat16)

    def dma(n):
        return pltpu.SemaphoreType.DMA((max(n, 1),))

    sems = []
    for send, recv in (
        (24, 24), (6, 6), (2 * dp * near, 2 * dp * near), (2 * dp * near, 2 * dp * near),
        (6, 6), (chunks, chunks),
        (chunks, chunks) if groups > 1 else (1, 1), (chunks, chunks * line),
        (chunks, chunks * line * sides), (chunks, chunks * line * max(1, turns // 2)),
        (chunks, chunks), (1, 1), (1, 1),
    ):
        sems += [dma(send), dma(recv)]
    vmem = pl.BlockSpec(memory_space=pltpu.VMEM)
    hbm = pl.BlockSpec(memory_space=pl.ANY)
    grad_weight, grad_bias, grad_head = pl.pallas_call(
        functools.partial(kernel, sizes, line),
        out_shape=(
            pltpu.VMEM((TAPS**3, chans, chans), jnp.float32),
            pltpu.VMEM((1, chans), jnp.float32),
            pltpu.VMEM((1, chans), jnp.float32),
        ),
        in_specs=[hbm, hbm, vmem, vmem],
        out_specs=(vmem, vmem, vmem),
        scratch_shapes=[
            pltpu.VMEM((TAPS**3, chans, chans), jnp.bfloat16),
            pltpu.VMEM((TAPS**3, chans, chans), jnp.bfloat16),
            pad, pad, pad,
            pltpu.VMEM((TAPS, count, chans), jnp.float32),
            field, field,
            gathered, gathered,
            pltpu.VMEM((2, frames, chans, cols), jnp.bfloat16),
            pltpu.VMEM((2, plane, frames + 2, share, cols), jnp.bfloat16),
            pltpu.VMEM((2, dp, rows + 2, frames + 2, TAPS * share, cols), jnp.bfloat16),
            pltpu.VMEM((TAPS, taps * share, chans), jnp.float32),
            pltpu.VMEM((chunks, line, taps, part, wide), jnp.float32),
            coded, coded,
            pltpu.VMEM((chunks, groups, taps + 1, part, wide), jnp.bfloat16),
            pltpu.VMEM((chunks, plane * line, taps + 1, part, wide), jnp.bfloat16),
            pltpu.VMEM((SUB, chans), jnp.float32),
            pltpu.VMEM((plane, SUB, chans), jnp.float32),
            pltpu.VMEM((tm, SUB, chans), jnp.float32),
            dma(3), *sems,
        ],
        compiler_params=pltpu.CompilerParams(
            collective_id=0, has_side_effects=True, vmem_limit_bytes=48 * 1024 * 1024
        ),
    )(
        pltpu.with_memory_space_constraint(clips.reshape(frames, cols, chans), pltpu.HBM),
        weight.reshape(TAPS**3, chans, chans),
        bias.reshape(1, chans),
        head.reshape(1, chans),
    )
    grad_weight = grad_weight.reshape(TAPS, TAPS, TAPS, chans, chans)
    return grad_weight, grad_bias.reshape(chans), grad_head.reshape(chans)


def solution(mesh):
    sizes = tuple(mesh.shape[axis] for axis in ("dp", "tm", "rows"))
    return jax.shard_map(
        functools.partial(per_device, sizes),
        mesh=mesh,
        in_specs=(P("dp", "tm", "rows", None, None), P(), P(), P()),
        out_specs=(P(), P(), P()),
        check_vma=False,
    )
```

time: 82.9 us -> 80.7 us (0.973)
  Pallas kernels: 78 us -> 75.8 us
    pallas_call x1, Pallas kernels: 78 us -> 75.8 us  [per_device(): pl.pallas_call(functools.partial(kernel, sizes, line), out_shape=(pltpu.V...]
where the time goes in v2:
time: 80.7 us; the launch traced here: 80.6 us
  Pallas kernels  75.8 us (94%)
  local copies, waits for them, and re-layouts  4.09 us (5%)
    pallas_call x1, Pallas kernels, per_device(): pl.pallas_call(functools.partial(kernel, sizes, line), out_shape=(pltpu.V...  75.8 us
    unnamed x3, local copies, waits for them, and re-layouts  4.09 us

profile of v2, /device:TPU:0, one launch (start us, length us, event | category | flops | bytes accessed | tf_op | source)
XLA Modules:
  0.0 80.6 jit_solution(11900457823198576710)
XLA Ops:
  0.6 75.8 %shard_map.67 = (f32[27,256,256]{2,1,0:T(8,128)S(1)}, f32[1,256]{1,0:T(1,128)S(1)}, f32[1,256]{1,0:T(1,128)S(1)}) custom-call(bf16[2,128,256]{2,1,0:T(8,128)(2,1)} %bitcast.11, bf16[27,256,256]{2,1,0:T(8,128)(2,1)} %bitcast.10, f32[1,256]{1,0:T(1,128)} %bitcast.12, f32[1,256]{1,0:T(1,128)} %bitcast.13), custom_call_target="tpu_custom_call" | custom-call | tf_op jit(solution)/shard_map/pallas_call | solution.py:779
  76.5 3.0 %copy.10 = f32[3,3,3,256,256]{4,3,2,1,0:T(8,128)} copy(f32[3,3,3,256,256]{4,3,2,1,0:T(8,128)S(1)} %bitcast.7) | data formatting | bytes 14155776
  79.4 0.6 copy.11
  80.0 0.6 copy.12

commit v3 on v2

--- a/solution.py
+++ b/solution.py
@@ -214,7 +214,7 @@
     def later(value):
         return jnp.where(column == cols - 1, 0.0, pltpu.roll(value, count - 1, 0))
 
-    def conv(which, pad, source, kernel_ref, idle, sent, side, between):
+    def conv(which, pad, source, kernel_ref, idle, sent, side, before, between):
         def put(shift_f, start, many, places, new=False):
             if not many:
                 return
@@ -247,6 +247,7 @@
         idle()
         side(which, pad, source)
         inner_frames((0, 2), False)
+        before()
         depth_wait(which, pad, source)
         between()
         outer_frames((1,))
@@ -310,27 +311,36 @@
             def _():
                 all_copy(which, buf, 0, 1).wait_send()
 
-    def relay_start(which, buf):
-        for i in others:
-            all_copy(which, buf, i, 1).start()
-        pass_copy(which, buf, 0, 1).start()
+    def far_copy(which, buf, i):
+        at = which * len(across) + across.index((i, 1))
+        block = buf.at[mine]
+        return remote(
+            block, block, all_send.at[at], all_recv.at[at],
+            device(dp=shift("dp", i), rows=mirror),
+        )
 
     def all_between(which, buf):
         if near == 2:
             @pl.when(edge)
             def _():
-                relay_start(which, buf)
-
+                for i in others:
+                    all_copy(which, buf, i, 1).start()
+                pass_copy(which, buf, 0, 1).start()
+
+    def all_outer(which, buf):
+        if near == 2:
             @pl.when(jnp.logical_not(edge))
             def _():
                 all_copy(which, buf, 0, 1).start()
+                for i in others:
+                    far_copy(which, buf, i).start()
 
     def all_relay(which, buf):
         if near == 2:
             @pl.when(jnp.logical_not(edge))
             def _():
                 all_copy(which, buf, 0, 1).wait_recv()
-                relay_start(which, buf)
+                pass_copy(which, buf, 0, 1).start()
 
     def all_near(which, buf):
         if near == 2:
@@ -450,7 +460,7 @@
     weight_copy.wait()
     pre = bias_ref[...] + conv(
         0, clip_pad, clips_ref, w_ref, turn_weight, lambda: all_sent(0, clip_all),
-        all_side(clip_all), lambda: all_between(0, clip_all),
+        all_side(clip_all), lambda: all_outer(0, clip_all), lambda: all_between(0, clip_all),
     )
     sig = jax.nn.sigmoid(pre)
     slope = sig * (1.0 + pre * (1.0 - sig))
@@ -466,7 +476,7 @@
 
     input_grad = conv(
         1, score_pad, score_own, wt_ref, lambda: None,
-        lambda: side_sent(1, score_pad, score_own), side_wait,
+        lambda: side_sent(1, score_pad, score_own), side_wait, lambda: None,
         lambda: slice_start(0, score_pad[pl.ds(1, frames), 1].astype(jnp.float32)),
     ).astype(jnp.bfloat16).reshape(frames, cols, chans)
     grad_pad[pl.ds(1, frames), 1] = input_grad
@@ -478,8 +488,9 @@
     all_far(0, clip_all, 1)
 
     back = penalty_weight * conv(
-        2, grad_pad, grad_own, w_ref, lambda: None, lambda: all_sent(1, grad_all),
-        all_side(grad_all), lambda: all_between(1, grad_all),
+        2, grad_pad, grad_own, w_ref, lambda: None,
+        lambda: (all_relay(1, grad_all), all_sent(1, grad_all)),
+        all_side(grad_all), lambda: all_outer(1, grad_all), lambda: all_between(1, grad_all),
     )
     pre_grad = back * head_ref[...] * curve_ref[...]
     slice_start(
@@ -500,7 +511,6 @@
         sum_copy(i, s).start()
 
     slice_end(0)
-    all_relay(1, grad_all)
     all_far(1, grad_all, 0)
     all_near(0, clip_all)
     all_end(0, clip_all)
@@ -546,8 +556,8 @@
             value, top = encode(total[c, along(step)])
             code[c, along(step), pl.ds(0, taps)] = value
             code[c, along(step), taps] = top
-        if c > 1 and line > 1:
-            part_all(c - 2).wait_send()
+        if c >= 1 and line > 1:
+            part_all(c - 1).wait_send()
         for step in range(line - 1, 0, -1):
             part_copy(c, step).start()
 
@@ -575,7 +585,7 @@
         value = total[c, inner]
         if line > 1:
             part_all(c).wait_recv()
-            if c >= len(chunks) - 2:
+            if c >= len(chunks) - 1:
                 part_all(c).wait_send()
         for step in range(1, line):
             value = value + decode(land[c, along(step)], taps)
@@ -604,12 +614,21 @@
             pair_copy(c, rank, 0).start()
 
     def take(c, rank):
-        line_copy(c, rank, inner).wait_recv()
         if rank > 1:
+            @pl.when(jnp.logical_not(middle))
+            def _():
+                line_copy(c, rank, inner).wait_recv()
+        else:
+            line_copy(c, rank, inner).wait_recv()
+        share_out(c, rank)
+
+    def onward(c):
+        if line == 4:
             @pl.when(middle)
             def _():
-                line_copy(c, rank, ranks[1]).start()
-        share_out(c, rank)
+                for rank in (2, 3):
+                    line_copy(c, rank, inner).wait_recv()
+                    line_copy(c, rank, ranks[1]).start()
 
     sides = [("rows", s) for s in range(1, near)] + [("dp", i) for i in range(1, dp)]
 
@@ -725,19 +744,38 @@
         bias_out[...] = value[0:1]
         head_out[...] = value[1:2]
 
-    pace = 1.77 * wide / LANES
+    pace = 2.65 * wide / LANES
     order = [(4.0, small_middle, ()), (16.0, small_end, ())]
     for c in range(len(chunks)):
-        got = 2.9 + pace + pace * c
-        order += [(pace * max(c - 1, 0), scatter, (c,)), (got, collect, (c,))]
+        got = 4.9 + pace * c
+        order += [
+            (got - 5.2 , scatter, (c,)), (got, collect, (c,)), (got + 4.5, onward, (c,)),
+            (got + 19.0, finish, (c,)),
+        ]
         for rank in range(line):
-            here = got + (0.0, 3.5, 5.0, 6.5)[rank]
             if rank:
-                order.append((here, take, (c, rank)))
-            order += [(here + 3.5, relay, (c, rank)), (here + 7.5, handover, (c, rank))]
-        order.append((got + 16.5, finish, (c,)))
+                order.append((got + (0, 4.4, 8.5, 8.5)[rank], take, (c, rank)))
+            order += [
+                (got + (4.6, 8.6, 12.5, 12.5)[rank], relay, (c, rank)), (got + (8.7, 12.6, 16.5, 16.5)[rank], handover, (c, rank)),
+            ]
     for _, stage, what in sorted(order, key=lambda entry: entry[0]):
         stage(*what)
+
+
+def put_out(grad_ref, bias_ref, head_ref, grad_out, bias_out, head_out, sem):
+    taps = TAPS**2
+    copies = [
+        pltpu.make_async_copy(
+            grad_ref.at[pl.ds(k * TAPS, TAPS)], grad_out.at[pl.ds(k * TAPS, TAPS)], sem.at[k]
+        )
+        for k in range(taps)
+    ]
+    copies.append(pltpu.make_async_copy(bias_ref, bias_out, sem.at[taps]))
+    copies.append(pltpu.make_async_copy(head_ref, head_out, sem.at[taps + 1]))
+    for copy in copies:
+        copy.start()
+    for copy in copies:
+        copy.wait()
 
 
 def per_device(sizes, clips, weight, bias, head):
@@ -814,6 +852,15 @@
         bias.reshape(1, chans),
         head.reshape(1, chans),
     )
+    row = jax.ShapeDtypeStruct((1, chans), jnp.float32)
+    grad_weight, grad_bias, grad_head = pl.pallas_call(
+        put_out,
+        out_shape=(jax.ShapeDtypeStruct((TAPS**3, chans, chans), jnp.float32), row, row),
+        in_specs=[vmem, vmem, vmem],
+        out_specs=(hbm, hbm, hbm),
+        scratch_shapes=[pltpu.SemaphoreType.DMA((TAPS**2 + 2,))],
+        compiler_params=pltpu.CompilerParams(vmem_limit_bytes=8 * 1024 * 1024),
+    )(grad_weight, grad_bias, grad_head)
     grad_weight = grad_weight.reshape(TAPS, TAPS, TAPS, chans, chans)
     return grad_weight, grad_bias.reshape(chans), grad_head.reshape(chans)
 

time: 80.7 us -> 73.5 us (0.911)
  local copies, waits for them, and re-layouts: 4.09 us -> 0 us
  Pallas kernels: 75.8 us -> 72.5 us
    pallas_call x1, Pallas kernels: 75.8 us -> 69.5 us  [per_device(): pl.pallas_call(functools.partial(kernel, sizes, line), out_shape=(pltpu.V...]
    unnamed x3 -> x0, local copies, waits for them, and re-layouts: 4.09 us -> none
    pallas_call x0 -> x1, Pallas kernels: none -> 3.01 us  [per_device(): pl.pallas_call(put_out, out_shape=(jax.ShapeDtypeStruct((TAPS ** 3, chans...]
where the time goes in v3:
time: 73.5 us; the launch traced here: 73.3 us
  Pallas kernels  72.5 us (99%)
  between operations  0.8 us (1%)
    pallas_call x1, Pallas kernels, per_device(): pl.pallas_call(functools.partial(kernel, sizes, line), out_shape=(pltpu.V...  69.5 us
    pallas_call x1, Pallas kernels, per_device(): pl.pallas_call(put_out, out_shape=(jax.ShapeDtypeStruct((TAPS ** 3, chans...  3.01 us

profile of v3, /device:TPU:0, one launch (start us, length us, event | category | flops | bytes accessed | tf_op | source)
XLA Modules:
  0.0 73.3 jit_solution(293584407334439387)
XLA Ops:
  0.6 69.5 %shard_map.67 = (f32[27,256,256]{2,1,0:T(8,128)S(1)}, f32[1,256]{1,0:T(1,128)S(1)}, f32[1,256]{1,0:T(1,128)S(1)}) custom-call(bf16[2,128,256]{2,1,0:T(8,128)(2,1)} %bitcast.8, bf16[27,256,256]{2,1,0:T(8,128)(2,1)} %bitcast.7, f32[1,256]{1,0:T(1,128)} %bitcast.9, f32[1,256]{1,0:T(1,128)} %bitcast.10), custom_call_target="tpu_custom_call" | custom-call | tf_op jit(solution)/shard_map/pallas_call | solution.py:817
  70.1 3.0 %shard_map.68 = (f32[27,256,256]{2,1,0:T(8,128)}, f32[1,256]{1,0:T(1,128)}, f32[1,256]{1,0:T(1,128)}) custom-call(f32[27,256,256]{2,1,0:T(8,128)S(1)} %get-tuple-element.9.grad_ref, f32[1,256]{1,0:T(1,128)S(1)} %get-tuple-element.10.bias_ref, f32[1,256]{1,0:T(1,128)S(1)} %get-tuple-element.11.head_ref), custom_call_target="tpu_custom_call" | custom-call | tf_op jit(solution)/shard_map/pallas_call | solution.py:856

commit v4 on v3

--- a/solution.py
+++ b/solution.py
@@ -89,22 +89,30 @@
             barrier, inc=1, device_id=(shift("dp", i), shift("tm", t), shift("rows", s)),
             device_id_type=MESH,
         )
-    for axis, bound, fill in (
-        ("rows", 0, lambda pad: pad.at[:, 0]), ("rows", rows - 1, lambda pad: pad.at[:, 2]),
-        ("tm", 0, lambda pad: pad.at[0]), ("tm", tm - 1, lambda pad: pad.at[frames + 1]),
-    ):
-        @pl.when(me[axis] == bound)
-        def _():
-            for pad in (clip_pad, score_pad, grad_pad):
-                at = fill(pad)
-                at[...] = jnp.zeros(at.shape, at.dtype)
-    for which in range(2):
-        for edge in (0, rows + 1):
-            shifts[which, :, edge] = jnp.zeros(shifts.shape[1:2] + shifts.shape[3:], shifts.dtype)
-        for edge, bound in ((0, 0), (frames + 1, tm - 1)):
-            @pl.when(me["tm"] == bound)
-            def _():
-                slices[which, :, edge] = jnp.zeros((plane, share, cols), slices.dtype)
+    def clear(pads):
+        for axis, bound, fill in (
+            ("rows", 0, lambda pad: pad.at[:, 0]), ("rows", rows - 1, lambda pad: pad.at[:, 2]),
+            ("tm", 0, lambda pad: pad.at[0]), ("tm", tm - 1, lambda pad: pad.at[frames + 1]),
+        ):
+            @pl.when(me[axis] == bound)
+            def _():
+                for pad in pads:
+                    at = fill(pad)
+                    at[...] = jnp.zeros(at.shape, at.dtype)
+
+    def clear_later():
+        clear((score_pad, grad_pad))
+        for which in range(2):
+            for rim in (0, rows + 1):
+                shifts[which, :, rim] = jnp.zeros(
+                    shifts.shape[1:2] + shifts.shape[3:], shifts.dtype
+                )
+            for rim, bound in ((0, 0), (frames + 1, tm - 1)):
+                @pl.when(me["tm"] == bound)
+                def _():
+                    slices[which, :, rim] = jnp.zeros((plane, share, cols), slices.dtype)
+
+    clear((clip_pad,))
     pl.semaphore_wait(barrier, len(steps))
 
     moves = [(t, r) for t in (-1, 0, 1) for r in (-1, 0, 1) if (t, r) != (0, 0)]
@@ -173,9 +181,13 @@
             def _():
                 halo_copy(which, pad, source, 0, r).wait_send()
 
-    def side_wait(which, pad, source):
+    def side_wait(which, pad, source, close):
         for r in (-1, 1):
-            @pl.when(inside(0, -r))
+            here = leaves(0, r, False)
+            if close:
+                here = jnp.logical_and(inside(0, -r), jnp.logical_not(here))
+
+            @pl.when(here)
             def _():
                 halo_copy(which, pad, source, 0, r).wait_recv()
 
@@ -201,6 +213,9 @@
                 @pl.when(leaves(t, r, False))
                 def _():
                     halo_copy(which, pad, source, t, r).wait_recv()
+
+    def hand_wait(which, pad):
+        for t in (-1, 1):
             if pair == 2:
                 @pl.when(inside(-t, 0))
                 def _():
@@ -214,9 +229,9 @@
     def later(value):
         return jnp.where(column == cols - 1, 0.0, pltpu.roll(value, count - 1, 0))
 
-    def conv(which, pad, source, kernel_ref, idle, sent, side, before, between):
+    def conv(which, pad, source, kernel_ref, idle, sent, side, before, after, between):
         def put(shift_f, start, many, places, new=False):
-            if not many:
+            if not many or not places:
                 return
             left = jnp.concatenate(
                 [
@@ -242,17 +257,23 @@
             put(0, 0, 1, places)
             put(2, frames - 1, 1, places)
 
+        close, far = ((1 + toward,), (1 - toward,)) if pair == 2 else ((), (0, 2))
         inner_frames((1,), True)
         corner_start(which, pad, source)
         idle()
-        side(which, pad, source)
-        inner_frames((0, 2), False)
+        side(which, pad, source, True)
+        inner_frames(close, False)
         before()
         depth_wait(which, pad, source)
+        outer_frames((1,))
+        hand_wait(which, pad)
+        outer_frames(close)
+        after()
+        side(which, pad, source, False)
         between()
-        outer_frames((1,))
+        inner_frames(far, False)
         corner_wait(which, pad, source)
-        outer_frames((0, 2))
+        outer_frames(far)
         sent()
         return earlier(acc[0]) + acc[1] + later(acc[2])
 
@@ -292,12 +313,12 @@
             all_copy(which, buf, i, 0).start()
 
     def all_side(buf):
-        def side(which, pad, source):
+        def side(which, pad, source, close):
             at = which // 2
-            if pair == 2:
+            if pair == 2 and close:
                 pass_copy(at, buf, 0, 0).wait_recv()
                 pad[pl.ds(1, frames), 1 + toward] = buf[me["dp"] * rows + partner]
-            if near == 2:
+            if near == 2 and not close:
                 @pl.when(edge)
                 def _():
                     all_copy(at, buf, 0, 1).wait_recv()
@@ -384,9 +405,11 @@
 
     pieces = [(i, s) for i in range(dp) for s in range(rows)]
 
-    def slice_start(which, value):
+    def slice_turn(which, value):
         for f in range(frames):
-            turned[which, f] = value[f].T.astype(jnp.bfloat16)
+            turned[which, f] = value[f].T
+
+    def slice_start(which):
         for t in (1, -1):
             @pl.when(inside(t, 0))
             def _():
@@ -451,6 +474,7 @@
             return carry
 
         lax.fori_loop(0, TAPS**3, one, 0, unroll=3)
+        clear_later()
 
     depth_start(0, clip_pad, clips_ref)
     clip_copy.wait()
@@ -460,7 +484,8 @@
     weight_copy.wait()
     pre = bias_ref[...] + conv(
         0, clip_pad, clips_ref, w_ref, turn_weight, lambda: all_sent(0, clip_all),
-        all_side(clip_all), lambda: all_outer(0, clip_all), lambda: all_between(0, clip_all),
+        all_side(clip_all), lambda: all_outer(0, clip_all), lambda: None,
+        lambda: all_between(0, clip_all),
     )
     sig = jax.nn.sigmoid(pre)
     slope = sig * (1.0 + pre * (1.0 - sig))
@@ -477,7 +502,8 @@
     input_grad = conv(
         1, score_pad, score_own, wt_ref, lambda: None,
         lambda: side_sent(1, score_pad, score_own), side_wait, lambda: None,
-        lambda: slice_start(0, score_pad[pl.ds(1, frames), 1].astype(jnp.float32)),
+        lambda: slice_turn(0, score_pad[pl.ds(1, frames), 1]),
+        lambda: slice_start(0),
     ).astype(jnp.bfloat16).reshape(frames, cols, chans)
     grad_pad[pl.ds(1, frames), 1] = input_grad
     grad_all[mine] = input_grad
@@ -490,12 +516,14 @@
     back = penalty_weight * conv(
         2, grad_pad, grad_own, w_ref, lambda: None,
         lambda: (all_relay(1, grad_all), all_sent(1, grad_all)),
-        all_side(grad_all), lambda: all_outer(1, grad_all), lambda: all_between(1, grad_all),
+        all_side(grad_all), lambda: all_outer(1, grad_all), lambda: None,
+        lambda: all_between(1, grad_all),
     )
     pre_grad = back * head_ref[...] * curve_ref[...]
-    slice_start(
-        1, pre_grad.astype(jnp.bfloat16).astype(jnp.float32).reshape(frames, cols, chans)
+    slice_turn(
+        1, pre_grad.astype(jnp.bfloat16).reshape(frames, cols, chans)
     )
+    slice_start(1)
     small_mine[...] = jnp.zeros_like(small_mine)
     small_mine[pl.ds(0, 1)] = jnp.sum(pre_grad, axis=0, keepdims=True)
     small_mine[pl.ds(1, 1)] = jnp.sum(back * slope_ref[...], axis=0, keepdims=True)
@@ -518,14 +546,10 @@
     for a in range(TAPS):
         first[a] = correlate(0, grad_all, a, [me["dp"]])
     all_far(1, grad_all, 1)
+    slice_end(1)
+    for a in range(TAPS):
+        first[a] = penalty_weight * first[a] + correlate(1, clip_all, a, range(dp))
     all_end(1, grad_all)
-    for a in range(TAPS):
-        first[a] = penalty_weight * (
-            first[a] + correlate(0, grad_all, a, [shift("dp", i) for i in others])
-            if dp > 1 else first[a]
-        )
-
-    slice_end(1)
     inner, outer = lax.rem(me["tm"], line), me["tm"] // line
     wide = full.shape[-1]
     chunks = [(a, low) for a in range(TAPS) for low in range(chans // wide)]
@@ -543,15 +567,20 @@
         block = land.at[c, pl.ds(0, line - 1)]
         return remote(block, block, part_send.at[c], part_recv.at[c], device())
 
+    def product(a):
+        both = first[a]
+        if dp > 1:
+            both = both + penalty_weight * correlate(
+                0, grad_all, a, [shift("dp", i) for i in others]
+            )
+        both = both.reshape(taps, share, chans)
+        for k in range(chans // wide):
+            for t in range(line):
+                total[a * (chans // wide) + k, t] = both[
+                    :, t * part : (t + 1) * part, k * wide : (k + 1) * wide
+                ]
+
     def scatter(c):
-        a, low = chunks[c]
-        if low == 0:
-            both = (first[a] + correlate(1, clip_all, a, range(dp))).reshape(taps, share, chans)
-            for k in range(chans // wide):
-                for t in range(line):
-                    total[c + k, t] = both[
-                        :, t * part : (t + 1) * part, k * wide : (k + 1) * wide
-                    ]
         for step in range(line - 1, 0, -1):
             value, top = encode(total[c, along(step)])
             code[c, along(step), pl.ds(0, taps)] = value
@@ -745,18 +774,20 @@
         head_out[...] = value[1:2]
 
     pace = 2.65 * wide / LANES
-    order = [(4.0, small_middle, ()), (16.0, small_end, ())]
+    order = [(4.0, small_middle, ()), (16.0, small_end, ()), (-9.0, product, (0,))]
+    order += [(got_a, product, (a,)) for a, got_a in ((1, 0.1), (2, 2.0))]
     for c in range(len(chunks)):
         got = 4.9 + pace * c
         order += [
-            (got - 5.2 , scatter, (c,)), (got, collect, (c,)), (got + 4.5, onward, (c,)),
-            (got + 19.0, finish, (c,)),
+            (got - 5.2, scatter, (c,)), (got, collect, (c,)), (got + 2.8, onward, (c,)),
+            (got + 23.0, finish, (c,)),
         ]
         for rank in range(line):
             if rank:
-                order.append((got + (0, 4.4, 8.5, 8.5)[rank], take, (c, rank)))
+                order.append((got + (0, 2.9, 5.4, 5.5)[rank], take, (c, rank)))
             order += [
-                (got + (4.6, 8.6, 12.5, 12.5)[rank], relay, (c, rank)), (got + (8.7, 12.6, 16.5, 16.5)[rank], handover, (c, rank)),
+                (got + (7.0, 10.0, 13.0, 13.1)[rank], relay, (c, rank)),
+                (got + (13.2, 16.0, 19.0, 19.1)[rank], handover, (c, rank)),
             ]
     for _, stage, what in sorted(order, key=lambda entry: entry[0]):
         stage(*what)

time: 73.5 us -> 72.2 us (0.982)
  Pallas kernels: 72.5 us -> 71.2 us
    pallas_call x1, Pallas kernels: 69.5 us -> 68.2 us  [per_device(): pl.pallas_call(functools.partial(kernel, sizes, line), out_shape=(pltpu.V...]
where the time goes in v4:
time: 72.2 us; the launch traced here: 72 us
  Pallas kernels  71.2 us (99%)
  between operations  0.8 us (1%)
    pallas_call x1, Pallas kernels, per_device(): pl.pallas_call(functools.partial(kernel, sizes, line), out_shape=(pltpu.V...  68.2 us
    pallas_call x1, Pallas kernels, per_device(): pl.pallas_call(put_out, out_shape=(jax.ShapeDtypeStruct((TAPS ** 3, chans...  3.01 us

profile of v4, /device:TPU:0, one launch (start us, length us, event | category | flops | bytes accessed | tf_op | source)
XLA Modules:
  0.0 72.0 jit_solution(7448593029367707331)
XLA Ops:
  0.6 68.2 %shard_map.67 = (f32[27,256,256]{2,1,0:T(8,128)S(1)}, f32[1,256]{1,0:T(1,128)S(1)}, f32[1,256]{1,0:T(1,128)S(1)}) custom-call(bf16[2,128,256]{2,1,0:T(8,128)(2,1)} %bitcast.8, bf16[27,256,256]{2,1,0:T(8,128)(2,1)} %bitcast.7, f32[1,256]{1,0:T(1,128)} %bitcast.9, f32[1,256]{1,0:T(1,128)} %bitcast.10), custom_call_target="tpu_custom_call" | custom-call | tf_op jit(solution)/shard_map/pallas_call | solution.py:848
  68.8 3.0 %shard_map.68 = (f32[27,256,256]{2,1,0:T(8,128)}, f32[1,256]{1,0:T(1,128)}, f32[1,256]{1,0:T(1,128)}) custom-call(f32[27,256,256]{2,1,0:T(8,128)S(1)} %get-tuple-element.9.grad_ref, f32[1,256]{1,0:T(1,128)S(1)} %get-tuple-element.10.bias_ref, f32[1,256]{1,0:T(1,128)S(1)} %get-tuple-element.11.head_ref), custom_call_target="tpu_custom_call" | custom-call | tf_op jit(solution)/shard_map/pallas_call | solution.py:887

commit v5 on v4

--- a/solution.py
+++ b/solution.py
@@ -786,7 +786,7 @@
             if rank:
                 order.append((got + (0, 2.9, 5.4, 5.5)[rank], take, (c, rank)))
             order += [
-                (got + (7.0, 10.0, 13.0, 13.1)[rank], relay, (c, rank)),
+                (got + (7.0, 10.0, 12.2, 12.3)[rank], relay, (c, rank)),
                 (got + (13.2, 16.0, 19.0, 19.1)[rank], handover, (c, rank)),
             ]
     for _, stage, what in sorted(order, key=lambda entry: entry[0]):
@@ -797,12 +797,12 @@
     taps = TAPS**2
     copies = [
         pltpu.make_async_copy(
-            grad_ref.at[pl.ds(k * TAPS, TAPS)], grad_out.at[pl.ds(k * TAPS, TAPS)], sem.at[k]
-        )
-        for k in range(taps)
+            grad_ref.at[pl.ds(k * taps, taps)], grad_out.at[pl.ds(k * taps, taps)], sem.at[k]
+        )
+        for k in range(TAPS)
     ]
-    copies.append(pltpu.make_async_copy(bias_ref, bias_out, sem.at[taps]))
-    copies.append(pltpu.make_async_copy(head_ref, head_out, sem.at[taps + 1]))
+    copies.append(pltpu.make_async_copy(bias_ref, bias_out, sem.at[TAPS]))
+    copies.append(pltpu.make_async_copy(head_ref, head_out, sem.at[TAPS + 1]))
     for copy in copies:
         copy.start()
     for copy in copies:
@@ -889,7 +889,7 @@
         out_shape=(jax.ShapeDtypeStruct((TAPS**3, chans, chans), jnp.float32), row, row),
         in_specs=[vmem, vmem, vmem],
         out_specs=(hbm, hbm, hbm),
-        scratch_shapes=[pltpu.SemaphoreType.DMA((TAPS**2 + 2,))],
+        scratch_shapes=[pltpu.SemaphoreType.DMA((TAPS + 2,))],
         compiler_params=pltpu.CompilerParams(vmem_limit_bytes=8 * 1024 * 1024),
     )(grad_weight, grad_bias, grad_head)
     grad_weight = grad_weight.reshape(TAPS, TAPS, TAPS, chans, chans)

time: 72.2 us -> 72.2 us (level)
  no operation moved by 1% of the time
where the time goes in v5:
time: 72.2 us; the launch traced here: 72 us
  Pallas kernels  71.2 us (99%)
  between operations  0.8 us (1%)
    pallas_call x1, Pallas kernels, per_device(): pl.pallas_call(functools.partial(kernel, sizes, line), out_shape=(pltpu.V...  68.2 us
    pallas_call x1, Pallas kernels, per_device(): pl.pallas_call(put_out, out_shape=(jax.ShapeDtypeStruct((TAPS ** 3, chans...  3.01 us

profile of v5, /device:TPU:0, one launch (start us, length us, event | category | flops | bytes accessed | tf_op | source)
XLA Modules:
  0.0 72.0 jit_solution(600732314294255287)
XLA Ops:
  0.6 68.2 %shard_map.67 = (f32[27,256,256]{2,1,0:T(8,128)S(1)}, f32[1,256]{1,0:T(1,128)S(1)}, f32[1,256]{1,0:T(1,128)S(1)}) custom-call(bf16[2,128,256]{2,1,0:T(8,128)(2,1)} %bitcast.8, bf16[27,256,256]{2,1,0:T(8,128)(2,1)} %bitcast.7, f32[1,256]{1,0:T(1,128)} %bitcast.9, f32[1,256]{1,0:T(1,128)} %bitcast.10), custom_call_target="tpu_custom_call" | custom-call | tf_op jit(solution)/shard_map/pallas_call | solution.py:848
  68.8 3.0 %shard_map.68 = (f32[27,256,256]{2,1,0:T(8,128)}, f32[1,256]{1,0:T(1,128)}, f32[1,256]{1,0:T(1,128)}) custom-call(f32[27,256,256]{2,1,0:T(8,128)S(1)} %get-tuple-element.9.grad_ref, f32[1,256]{1,0:T(1,128)S(1)} %get-tuple-element.10.bias_ref, f32[1,256]{1,0:T(1,128)S(1)} %get-tuple-element.11.head_ref), custom_call_target="tpu_custom_call" | custom-call | tf_op jit(solution)/shard_map/pallas_call | solution.py:887
